TPU v7x, 16 devices: a 4x2x1 block of a 4x4x8 slice. The times are simulated.
16 devices in a mesh: rep: 2 (over y, z), dp: 8 (over x, core).
Axes of the slice: x: 4, y: 2, z: 1, core: 2. Of those that a mesh axis runs over, the one named last changes fastest.
The devices are a block of a 4x4x8 slice.
Arguments:
- x: bfloat16 [16, 2048, 896], P(('rep', 'dp')), parts along dimension 0
- dy: bfloat16 [16, 2048, 896], P(('rep', 'dp')), parts along dimension 0
- w_gate: bfloat16 [2, 896, 2304], replicated
- w_up: bfloat16 [2, 896, 2304], replicated
- w_down: bfloat16 [2, 2304, 896], replicated
- m_w_gate: float32 [2, 896, 2304], replicated
- m_w_up: float32 [2, 896, 2304], replicated
- m_w_down: float32 [2, 2304, 896], replicated
- v_w_gate: float32 [2, 896, 2304], replicated
- v_w_up: float32 [2, 896, 2304], replicated
- v_w_down: float32 [2, 2304, 896], replicated
Outputs:
- output 1: bfloat16 [4, 896, 2304], P('rep'), parts along dimension 0
- output 2: bfloat16 [4, 896, 2304], P('rep'), parts along dimension 0
- output 3: bfloat16 [4, 2304, 896], P('rep'), parts along dimension 0
- output 4: float32 [4, 896, 2304], P('rep'), parts along dimension 0
- output 5: float32 [4, 896, 2304], P('rep'), parts along dimension 0
- output 6: float32 [4, 2304, 896], P('rep'), parts along dimension 0
- output 7: float32 [4, 896, 2304], P('rep'), parts along dimension 0
- output 8: float32 [4, 896, 2304], P('rep'), parts along dimension 0
- output 9: float32 [4, 2304, 896], P('rep'), parts along dimension 0
There are 2 independent parts. A program takes and returns all parts, laid end to end along the dimension named above; an argument that names none is the same for every part.
All inputs are finite; a program needn't handle non-finite values.
Results may differ from a plain program's by a relative error of at most 0.02.
Values are sent between devices in bfloat16 or wider.
A program may use at most 768 MiB of HBM per device.

v0:
```python
import functools

import jax
import jax.numpy as jnp
from jax import lax
from jax.experimental import pallas as pl
from jax.experimental.pallas import tpu as pltpu
from jax.sharding import PartitionSpec as P


F32, BF16 = jnp.float32, jnp.bfloat16
PARAMS = functools.partial(pltpu.CompilerParams, vmem_limit_bytes=60 * 2**20)


def mm(a, b, ca=1, cb=0):
    return lax.dot_general(a, b, (((ca,), (cb,)), ((), ())), preferred_element_type=F32)


def normed(wide):
    scale = lax.rsqrt(jnp.mean(wide * wide, -1, keepdims=True) + 1e-6)
    return (wide * scale).astype(BF16)


def sigmoid(x):
    return 0.5 * jnp.tanh(0.5 * x) + 0.5


def cost(flops, nbytes):
    return pl.CostEstimate(flops=int(flops), bytes_accessed=int(nbytes), transcendentals=0)


def whole(shape):
    return pl.BlockSpec(shape, lambda *_: (0,) * len(shape), pipeline_mode=pl.Buffered(1))


def layer_of(array, number):
    return pl.BlockSpec((None, *array.shape[1:]), lambda *_: (number, 0, 0), pipeline_mode=pl.Buffered(1))


def chunks(ff, width):
    return [slice(i, i + width) for i in range(0, ff, width)]


def forward_kernel(width, h_ref, wg_ref, wu_ref, wd_ref, o_ref, hid_ref):
    wide = h_ref[...].astype(F32)
    a = normed(wide)
    for c in chunks(wg_ref.shape[1], width):
        gate, up = mm(a, wg_ref[:, c]), mm(a, wu_ref[:, c])
        hid_ref[:, c] = (gate * sigmoid(gate) * up).astype(BF16)
    y = mm(hid_ref[...], wd_ref[...]).astype(BF16).astype(F32)
    o_ref[...] = (wide + y).astype(BF16)


def forward(number, h, wg, wu, wd, tile=512, width=768):
    tokens, d = h.shape
    ff = wg.shape[2]
    return pl.pallas_call(
        functools.partial(forward_kernel, width),
        name="forward",
        grid=(tokens // tile,),
        in_specs=[pl.BlockSpec((tile, d), lambda i: (i, 0)), layer_of(wg, number), layer_of(wu, number), layer_of(wd, number)],
        out_specs=pl.BlockSpec((tile, d), lambda i: (i, 0)),
        out_shape=jax.ShapeDtypeStruct((tokens, d), BF16),
        scratch_shapes=[pltpu.VMEM((tile, ff), BF16)],
        compiler_params=PARAMS(),
        cost_estimate=cost(6 * tokens * d * ff, 2 * (2 * tokens * d + 3 * d * ff)),
    )(h, wg, wu, wd)


PAIRED, PASSED, ARRIVED = 2, 4, 6


def gradients_kernel(size, tile, h_ref, dy_ref, wg_ref, wu_ref, wd_ref, o_ref, *refs):
    *kept, a, x, y, g, pr, p, r1a, r1b, r2a, r2b, send, recv = refs
    step = pl.program_id(0)
    steps = pl.num_programs(0) - ARRIVED // 3
    pieces = 3 * steps
    slots = g.shape[0]
    rows = g.shape[1] // size
    width = g.shape[2]
    a_half, b_half = pl.ds(0, width // 2), pl.ds(width // 2, width // 2)
    quarters = size // 2
    me = lax.axis_index("dp")
    core, chip = lax.rem(me, 2), me // 2
    partner = me + 1 - 2 * core
    right, left = lax.rem(me + 2, size), lax.rem(me + size - 2, size)

    def of_chip(offset):
        return pl.ds(pl.multiple_of(lax.rem(chip + offset, quarters) * rows, 16), rows)

    def half(which):
        return pl.ds(pl.multiple_of(which * quarters * rows, 16), quarters * rows)

    def copy(kind, j, source, target, device):
        return pltpu.make_async_remote_copy(
            src_ref=source,
            dst_ref=target.at[j],
            send_sem=send.at[kind, j],
            recv_sem=recv.at[kind, j],
            device_id={"dp": device},
            device_id_type=pl.DeviceIdType.MESH,
        )

    def to_partner(j):
        return copy(0, j, g.at[lax.rem(j, slots), half(1 - core)], pr, partner)

    def first(j):
        opposite = of_chip(2)
        return copy(1, j, p.at[j, opposite, a_half], r1a, right), copy(2, j, p.at[j, opposite, b_half], r1b, left)

    def second(j):
        return copy(3, j, p.at[j, of_chip(1)], r2a, right), copy(4, j, p.at[j, of_chip(quarters - 1)], r2b, left)

    @pl.when(step == 0)
    def _():
        barrier = pltpu.get_barrier_semaphore()
        for device in (partner, left, right):
            pl.semaphore_signal(barrier, inc=1, device_id={"dp": device}, device_id_type=pl.DeviceIdType.MESH)
        pl.semaphore_wait(barrier, 3)
        for i in range(0, a.shape[0], tile):
            part = normed(h_ref[i : i + tile].astype(F32))
            a[i : i + tile] = part
            x[0, :, i : i + tile] = dy_ref[i : i + tile].T
            x[1, :, i : i + tile] = part.T

    @pl.when(step < steps)
    def _():
        for i in range(0, a.shape[0], tile):
            t = slice(i, i + tile)
            gate, up = mm(a[t], wg_ref[...]), mm(a[t], wu_ref[...])
            by_hid = mm(dy_ref[t], wd_ref[...], 1, 1).astype(BF16).astype(F32)
            s = sigmoid(gate)
            silu = gate * s
            y[0, t] = (silu * up).astype(BF16)
            dg = (by_hid * up * (s + silu * (1.0 - s))).astype(BF16)
            du = (by_hid * silu).astype(BF16)
            y[1, t] = dg
            y[2, t] = du
            if kept:
                kept[0][0, t] = dg
                kept[0][1, t] = du

    @pl.loop(0, 3)
    def _(which):
        k = 3 * step + which

        def stage(after):
            return pl.when((k >= after) & (k < pieces + after))

        @stage(0)
        def _():
            g[lax.rem(k, slots)] = mm(x[jnp.minimum(which, 1)], y[which]).astype(BF16)

        @stage(PAIRED)
        def _():
            j = k - PAIRED
            to_partner(j).wait()
            p[j] = (g[lax.rem(j, slots), half(core)].astype(F32) + pr[j].astype(F32)).astype(BF16)

        @stage(PASSED)
        def _():
            j = k - PASSED
            for one in first(j):
                one.wait()
            p[j, of_chip(1), a_half] = (p[j, of_chip(1), a_half].astype(F32) + r1a[j].astype(F32)).astype(BF16)
            p[j, of_chip(quarters - 1), b_half] = (p[j, of_chip(quarters - 1), b_half].astype(F32) + r1b[j].astype(F32)).astype(BF16)

        @stage(ARRIVED)
        def _():
            j = k - ARRIVED
            for one in second(j):
                one.wait()
            total = (p[j, of_chip(0)].astype(F32) + r2a[j].astype(F32) + r2b[j].astype(F32)).astype(BF16)
            o_ref[lax.rem(j, 3), :, pl.ds(pl.multiple_of((j // 3) * width, 128), width)] = total

        @stage(PASSED)
        def _():
            for one in second(k - PASSED):
                one.start()

        @stage(PAIRED)
        def _():
            for one in first(k - PAIRED):
                one.start()

        @stage(0)
        def _():
            to_partner(k).start()


def gradients(size, number, h, dy, wg, wu, wd, keep, width=256, tile=512):
    tokens, d = h.shape
    ff = wg.shape[2]
    steps, rows, half = ff // width, d // size, d // 2
    pieces = 3 * steps

    def now(k):
        return jnp.minimum(k, steps - 1)

    column = pl.BlockSpec((None, d, width), lambda k: (number, 0, now(k)))
    out_specs, out_shape = [whole((3, rows, ff))], [jax.ShapeDtypeStruct((3, rows, ff), BF16)]
    if keep:
        out_specs += [pl.BlockSpec((2, tokens, width), lambda k: (0, 0, now(k)))]
        out_shape += [jax.ShapeDtypeStruct((2, tokens, ff), BF16)]
    return pl.pallas_call(
        functools.partial(gradients_kernel, size, tile),
        name="gradients",
        grid=(steps + ARRIVED // 3,),
        in_specs=[whole((tokens, d))] * 2 + [column, column, pl.BlockSpec((None, width, d), lambda k: (number, now(k), 0))],
        out_specs=out_specs,
        out_shape=out_shape,
        scratch_shapes=[
            pltpu.VMEM((tokens, d), BF16),
            pltpu.VMEM((2, d, tokens), BF16),
            pltpu.VMEM((3, tokens, width), BF16),
            pltpu.VMEM((PAIRED + 1, d, width), BF16),
            pltpu.VMEM((pieces, half, width), BF16),
            pltpu.VMEM((pieces, half, width), BF16),
            pltpu.VMEM((pieces, rows, width // 2), BF16),
            pltpu.VMEM((pieces, rows, width // 2), BF16),
            pltpu.VMEM((pieces, rows, width), BF16),
            pltpu.VMEM((pieces, rows, width), BF16),
            pltpu.SemaphoreType.DMA((5, pieces)),
            pltpu.SemaphoreType.DMA((5, pieces)),
        ],
        compiler_params=PARAMS(collective_id=number, has_side_effects=True),
        cost_estimate=cost(18 * tokens * d * ff, 2 * (2 * tokens * d + 2 * tokens * ff + 6 * d * ff)),
    )(h, dy, wg, wu, wd)


def back_kernel(h_ref, dy_ref, dg_ref, du_ref, wg_ref, wu_ref, o_ref):
    by_a = mm(dg_ref[...], wg_ref[...], 1, 1).astype(BF16).astype(F32)
    by_a = (by_a + mm(du_ref[...], wu_ref[...], 1, 1).astype(BF16).astype(F32)).astype(BF16).astype(F32)
    wide = h_ref[...].astype(F32)
    scale = lax.rsqrt(jnp.mean(wide * wide, -1, keepdims=True) + 1e-6)
    by_h = scale * by_a - wide * (scale * scale * scale * jnp.mean(by_a * wide, -1, keepdims=True))
    o_ref[...] = (dy_ref[...].astype(F32) + by_h.astype(BF16).astype(F32)).astype(BF16)


def back(number, h, dy, y, wg, wu, tile=512):
    tokens, d = h.shape
    ff = wg.shape[2]
    row = pl.BlockSpec((tile, d), lambda i: (i, 0))
    by_gate, by_up = (pl.BlockSpec((None, tile, ff), lambda i, which=which: (which, i, 0)) for which in (0, 1))
    return pl.pallas_call(
        back_kernel,
        name="back",
        grid=(tokens // tile,),
        in_specs=[row, row, by_gate, by_up, layer_of(wg, number), layer_of(wu, number)],
        out_specs=row,
        out_shape=jax.ShapeDtypeStruct((tokens, d), BF16),
        compiler_params=PARAMS(),
        cost_estimate=cost(4 * tokens * d * ff, 2 * (3 * tokens * d + 2 * d * ff + 2 * tokens * ff)),
    )(h, dy, y, y, wg, wu)


def adamw_step(g, w_ref, m_ref, v_ref, ow_ref, om_ref, ov_ref):
    g = g.astype(F32)
    m = 0.9 * m_ref[...] + 0.1 * g
    v = 0.95 * v_ref[...] + 0.05 * g * g
    w = w_ref[...].astype(F32)
    ow_ref[...] = (w - 0.02 * (m * lax.rsqrt(v + 1e-8) + 0.1 * w)).astype(BF16)
    om_ref[...] = m
    ov_ref[...] = v


def adamw_kernel(place_ref, w_ref, m_ref, v_ref, *refs):
    parts, outs = refs[:10], refs[-3:]
    for which in range(8):

        @pl.when(pl.program_id(0) == which)
        def _(which=which):
            group = parts[5 * (which // 4) :]
            at = which % 4
            g = group[at][...] if at < 3 else jnp.concatenate([group[3][...], group[4][...]], 1)
            adamw_step(g, w_ref, m_ref, v_ref, *outs)


def adamw_turned_kernel(place_ref, w_ref, m_ref, v_ref, *refs):
    parts, outs, g_ref = refs[:10], refs[-4:-1], refs[-1]
    rows = parts[0].shape[0]
    early = pl.program_id(0) < pl.num_programs(0) // 2

    def put(which, value):
        g_ref[pl.ds(pl.multiple_of(place_ref[which] * rows, 16), rows)] = value

    for which in range(8):
        group = parts[5 * (which // 4) :]
        at = which % 4
        if at < 3:
            put(which, group[at][...])
        else:
            put(which, jnp.where(early, group[3][...], group[4][...]))
    adamw_step(g_ref[...].T, w_ref, m_ref, v_ref, *outs)


def adamw(place, number, at, parts, w, m, v, turned, so_far, width=384):
    rows, ff = parts[0].shape[1:]
    d = rows * place.shape[0]
    so_far = so_far or ()
    if turned:
        steps, kernel = ff // width, adamw_turned_kernel
        per = steps // 2
        big = pl.BlockSpec((None, width, d), lambda i, place: (number, i, 0))
        three = [pl.BlockSpec((None, rows, width), lambda i, place: (at, 0, i))] * 3
        three += [pl.BlockSpec((None, rows, width), lambda i, place: (at, 0, jnp.minimum(i, per - 1)))]
        three += [pl.BlockSpec((None, rows, width), lambda i, place: (at, 0, jnp.maximum(i - per, 0)))]
        scratch = [pltpu.VMEM((d, width), BF16)]
    else:
        steps, kernel = place.shape[0], adamw_kernel
        big = pl.BlockSpec((None, rows, ff), lambda i, place: (number, place[i], 0))
        three = [pl.BlockSpec((None, *part.shape[1:]), lambda i, place: (at, 0, 0), pipeline_mode=pl.Buffered(1)) for part in parts[:5]]
        scratch = []
    return pl.pallas_call(
        kernel,
        name="adamw",
        grid_spec=pltpu.PrefetchScalarGridSpec(
            num_scalar_prefetch=1,
            grid=(steps,),
            in_specs=[big, big, big, *three, *three, *[pl.BlockSpec(memory_space=pl.ANY)] * len(so_far)],
            out_specs=[big] * 3,
            scratch_shapes=scratch,
        ),
        out_shape=[jax.ShapeDtypeStruct(w.shape, BF16), jax.ShapeDtypeStruct(m.shape, F32), jax.ShapeDtypeStruct(v.shape, F32)],
        input_output_aliases={14 + i: i for i in range(len(so_far))},
        compiler_params=PARAMS(),
        cost_estimate=cost(5 * 2048 * d * ff // 2, 22 * d * ff),
    )(place, w, m, v, *parts, *so_far)


def solution(mesh):
    size = mesh.shape["dp"]
    swap = [(i, i ^ 1) for i in range(size)]
    to_right = [(i, (i + 2) % size) for i in range(size)]
    to_left = [(i, (i - 2) % size) for i in range(size)]

    def step(x, dy, *arrays):
        weights, moments, squares = (arrays[i : i + 3] for i in (0, 3, 6))
        layers = weights[0].shape[0]
        me = lax.axis_index("dp")
        core, chip = me % 2, me // 2
        offsets = jnp.array([0, size // 2 - 1, 1, 2], jnp.int32)
        place = ((chip + offsets) % (size // 2))[None] + jnp.stack([core, 1 - core])[:, None] * (size // 2)
        place = place.reshape(-1).astype(jnp.int32)

        def hop(one, to):
            return lax.ppermute(one, "dp", to)

        def gathered(own):
            middle = own.shape[2] // 2
            left, right = hop(own, to_right), hop(own, to_left)
            first = hop(left[:, :, :middle], to_right)
            second = hop(right[:, :, middle:], to_left)
            pairs = [hop(own, swap), hop(left, swap), hop(right, swap)]
            pairs += [hop(first, swap), hop(second, swap)]
            return (own, left, right, first, second, *pairs)

        h, kept = x[0], []
        for number in range(layers):
            kept.append(h)
            if number < layers - 1:
                h = forward(number, h, *weights)
        by_h, out, sums = dy[0], [None] * 3, []
        for number in reversed(range(layers)):
            own, *by_both = gradients(size, number, kept[number], by_h, *weights, number > 0)
            parts = gathered(own)
            for at, which in enumerate((2, 0, 1)):
                sums.append((number, which, at, parts))
            if number:
                by_h = back(number, kept[number], by_h, by_both[0], *weights[:2])
        for number, which, at, parts in sums:
            out[which] = adamw(place, number, at, parts, weights[which], moments[which], squares[which], which == 2, out[which])
        return tuple(one[which] for which in range(3) for one in out)

    return jax.shard_map(
        step,
        mesh=mesh,
        in_specs=(P(("rep", "dp"), None, None),) * 2 + (P(None, None, None),) * 9,
        out_specs=(P("rep", None, None),) * 9,
        check_vma=False,
    )
```

profile of v0, /device:TPU:112, one launch (start us, length us, event | category | flops | bytes accessed | tf_op | source)
XLA Modules:
  0.0 507.7 jit_solution(7554850483368590746)
XLA Ops:
  0.6 36.6 %forward.1.h_ref = bf16[2048,896]{1,0:T(8,128)(2,1)} custom-call(bf16[2048,896]{1,0:T(8,128)(2,1)} %bitcast.6, bf16[2,896,2304]{2,1,0:T(8,128)(2,1)} %w_ref.7, bf16[2,896,2304]{2,1,0:T(8,128)(2,1)} %w_ref.9, bf16[2,2304,896]{2,1,0:T(8,128)(2,1)} %w_ref.11), custom_call_target="tpu_custom_call" | custom-call | flops 25367150592 | bytes 19726336 | tf_op jit(solution)/shard_map/forward/pallas_call | solution.py:57
  37.2 107.5 %gradients.2 = (bf16[3,112,2304]{2,1,0:T(8,128)(2,1)}, bf16[2,2048,2304]{2,1,0:T(8,128)(2,1)}) custom-call(bf16[2048,896]{1,0:T(8,128)(2,1)} %forward.1.h_ref, bf16[2048,896]{1,0:T(8,128)(2,1)} %bitcast.4, bf16[2,896,2304]{2,1,0:T(8,128)(2,1)} %w_ref.7, bf16[2,896,2304]{2,1,0:T(8,128)(2,1)} %w_ref.9, bf16[2,2304,896]{2,1,0:T(8,128)(2,1)} %w_ref.11), custom_call_target="tpu_custom_call" | custom-call | flops 76101451776 | bytes 50987008 | tf_op jit(solution)/shard_map/gradients/pallas_call | solution.py:205
  144.7 29.4 %back.1.dy_ref = bf16[2048,896]{1,0:T(8,128)(2,1)} custom-call(bf16[2048,896]{1,0:T(8,128)(2,1)} %forward.1.h_ref, bf16[2048,896]{1,0:T(8,128)(2,1)} %bitcast.5, bf16[2,2048,2304]{2,1,0:T(8,128)(2,1)} %get-tuple-element.29.dg_ref.du_ref, bf16[2,2048,2304]{2,1,0:T(8,128)(2,1)} %get-tuple-element.29.dg_ref.du_ref, bf16[2,896,2304]{2,1,0:T(8,128)(2,1)} %w_ref.7, ...), custom_call_target="tpu_custom_call" | custom-call | flops 16911433728 | bytes 38141952 | tf_op jit(solution)/shard_map/back/pallas_call | solution.py:245
  174.1 104.3 %gradients.3.refs_0_ = bf16[3,112,2304]{2,1,0:T(8,128)(2,1)} custom-call(bf16[2048,896]{1,0:T(8,128)(2,1)} %bitcast.7, bf16[2048,896]{1,0:T(8,128)(2,1)} %back.1.dy_ref, bf16[2,896,2304]{2,1,0:T(8,128)(2,1)} %w_ref.7, bf16[2,896,2304]{2,1,0:T(8,128)(2,1)} %w_ref.9, bf16[2,2304,896]{2,1,0:T(8,128)(2,1)} %w_ref.11), custom_call_target="tpu_custom_call" | custom-call | flops 76101451776 | bytes 50987008 | tf_op jit(solution)/shard_map/gradients/pallas_call | solution.py:205
  278.4 2.0 collective-permute-start.1
  280.4 0.1 collective-permute-start.10
  280.5 1.9 collective-permute-start.9
  282.5 32.9 %collective-permute-done.1.refs_2_ = bf16[3,112,2304]{2,1,0:T(8,128)(2,1)S(1)} collective-permute-done((bf16[3,112,2304]{2,1,0:T(8,128)(2,1)}, bf16[3,112,2304]{2,1,0:T(8,128)(2,1)S(1)}, u32[]{:S(2)}, u32[]{:S(2)}) %collective-permute-start.1) | collective-permute-done | bytes 1548320 | tf_op jit(solution)/shard_map/ppermute | solution.py:347
  315.5 3.2 collective-permute-start.3
  318.7 30.0 %collective-permute-done.10.refs_2_ = bf16[3,112,2304]{2,1,0:T(8,128)(2,1)} collective-permute-done((bf16[3,112,2304]{2,1,0:T(8,128)(2,1)}, bf16[3,112,2304]{2,1,0:T(8,128)(2,1)}, u32[]{:S(2)}, u32[]{:S(2)}) %collective-permute-start.10) | collective-permute-done | bytes 1548320 | tf_op jit(solution)/shard_map/ppermute | solution.py:347
  348.7 1.2 slice.19
  349.9 3.2 collective-permute-start.12
  353.1 1.2 slice.18
  354.4 0.1 collective-permute-start.11
  354.5 0.6 collective-permute-start.14
  355.0 0.9 slice.16
  356.0 9.3 %collective-permute-done.3.refs_4_ = bf16[3,112,1152]{2,1,0:T(8,128)(2,1)} collective-permute-done((bf16[3,112,1152]{2,1,0:T(8,128)(2,1)S(1)}, bf16[3,112,1152]{2,1,0:T(8,128)(2,1)}, u32[]{:S(2)}, u32[]{:S(2)}) %collective-permute-start.3) | collective-permute-done | bytes 774176 | tf_op jit(solution)/shard_map/ppermute | solution.py:347
  365.3 0.7 collective-permute-start.2
  366.0 11.3 %collective-permute-done.12.refs_4_ = bf16[3,112,1152]{2,1,0:T(8,128)(2,1)} collective-permute-done((bf16[3,112,1152]{2,1,0:T(8,128)(2,1)S(1)}, bf16[3,112,1152]{2,1,0:T(8,128)(2,1)}, u32[]{:S(2)}, u32[]{:S(2)}) %collective-permute-start.12) | collective-permute-done | bytes 774176 | tf_op jit(solution)/shard_map/ppermute | solution.py:347
  377.4 0.5 collective-permute-start.16
  377.9 0.1 add_multiply_fusion
  378.0 0.6 add.41.place_ref
  378.7 13.4 %collective-permute-done.2.refs_3_ = bf16[3,112,1152]{2,1,0:T(8,128)(2,1)} collective-permute-done((bf16[3,112,1152]{2,1,0:T(8,128)(2,1)}, bf16[3,112,1152]{2,1,0:T(8,128)(2,1)}, u32[]{:S(2)}, u32[]{:S(2)}) %collective-permute-start.2) | collective-permute-done | bytes 774176 | tf_op jit(solution)/shard_map/ppermute | solution.py:347
  392.0 0.5 collective-permute-start.6
  392.6 0.4 collective-permute-start.8
  393.1 17.7 %adamw.10 = (bf16[2,2304,896]{2,1,0:T(8,128)(2,1)}, f32[2,2304,896]{2,1,0:T(8,128)}, f32[2,2304,896]{2,1,0:T(8,128)}) custom-call(s32[8]{0:T(128)} %add.41.place_ref, bf16[2,2304,896]{2,1,0:T(8,128)(2,1)} %w_ref.11, f32[2,2304,896]{2,1,0:T(8,128)} %m_ref.11, f32[2,2304,896]{2,1,0:T(8,128)} %v_ref.11, bf16[3,112,2304]{2,1,0:T(8,128)(2,1)} %get-tuple-element.30.refs_0_, ...), custom_call_target="tpu_custom_call" | custom-call | flops 10569646080 | bytes 45416448 | tf_op jit(solution)/shard_map/adamw/pallas_call | solution.py:314
  410.9 19.3 %adamw.8 = (bf16[2,896,2304]{2,1,0:T(8,128)(2,1)}, f32[2,896,2304]{2,1,0:T(8,128)}, f32[2,896,2304]{2,1,0:T(8,128)}) custom-call(s32[8]{0:T(128)} %add.41.place_ref, bf16[2,896,2304]{2,1,0:T(8,128)(2,1)} %w_ref.9, f32[2,896,2304]{2,1,0:T(8,128)} %m_ref.9, f32[2,896,2304]{2,1,0:T(8,128)} %v_ref.9, bf16[3,112,2304]{2,1,0:T(8,128)(2,1)} %get-tuple-element.30.refs_0_, ...), custom_call_target="tpu_custom_call" | custom-call | flops 10569646080 | bytes 45416448 | tf_op jit(solution)/shard_map/adamw/pallas_call | solution.py:314
  430.2 19.6 %adamw.6 = (bf16[2,896,2304]{2,1,0:T(8,128)(2,1)}, f32[2,896,2304]{2,1,0:T(8,128)}, f32[2,896,2304]{2,1,0:T(8,128)}) custom-call(s32[8]{0:T(128)} %add.41.place_ref, bf16[2,896,2304]{2,1,0:T(8,128)(2,1)} %w_ref.7, f32[2,896,2304]{2,1,0:T(8,128)} %m_ref.7, f32[2,896,2304]{2,1,0:T(8,128)} %v_ref.7, bf16[3,112,2304]{2,1,0:T(8,128)(2,1)} %get-tuple-element.30.refs_0_, ...), custom_call_target="tpu_custom_call" | custom-call | flops 10569646080 | bytes 45416448 | tf_op jit(solution)/shard_map/adamw/pallas_call | solution.py:314
  449.9 0.8 copy-done.2
  450.7 17.7 %adamw.11 = (bf16[2,2304,896]{2,1,0:T(8,128)(2,1)}, f32[2,2304,896]{2,1,0:T(8,128)}, f32[2,2304,896]{2,1,0:T(8,128)}) custom-call(s32[8]{0:T(128)} %add.41.place_ref, bf16[2,2304,896]{2,1,0:T(8,128)(2,1)} %w_ref.11, f32[2,2304,896]{2,1,0:T(8,128)} %m_ref.11, f32[2,2304,896]{2,1,0:T(8,128)} %v_ref.11, ...), custom_call_target="tpu_custom_call", output_to_operand_aliasing={{0}: (14, {}), {1}: (15, {}), {2}: (16, {})} | custom-call | flops 10569646080 | bytes 45416448 | tf_op jit(solution)/shard_map/adamw/pallas_call | solution.py:314
  468.4 19.3 %adamw.9 = (bf16[2,896,2304]{2,1,0:T(8,128)(2,1)}, f32[2,896,2304]{2,1,0:T(8,128)}, f32[2,896,2304]{2,1,0:T(8,128)}) custom-call(s32[8]{0:T(128)} %add.41.place_ref, bf16[2,896,2304]{2,1,0:T(8,128)(2,1)} %w_ref.9, f32[2,896,2304]{2,1,0:T(8,128)} %m_ref.9, f32[2,896,2304]{2,1,0:T(8,128)} %v_ref.9, ...), custom_call_target="tpu_custom_call", output_to_operand_aliasing={{0}: (14, {}), {1}: (15, {}), {2}: (16, {})} | custom-call | flops 10569646080 | bytes 45416448 | tf_op jit(solution)/shard_map/adamw/pallas_call | solution.py:314
  487.8 19.8 %adamw.7 = (bf16[2,896,2304]{2,1,0:T(8,128)(2,1)}, f32[2,896,2304]{2,1,0:T(8,128)}, f32[2,896,2304]{2,1,0:T(8,128)}) custom-call(s32[8]{0:T(128)} %add.41.place_ref, bf16[2,896,2304]{2,1,0:T(8,128)(2,1)} %w_ref.7, f32[2,896,2304]{2,1,0:T(8,128)} %m_ref.7, f32[2,896,2304]{2,1,0:T(8,128)} %v_ref.7, ...), custom_call_target="tpu_custom_call", output_to_operand_aliasing={{0}: (14, {}), {1}: (15, {}), {2}: (16, {})} | custom-call | flops 10569646080 | bytes 45416448 | tf_op jit(solution)/shard_map/adamw/pallas_call | solution.py:314
  (30 shorter events, 0.4 us)
Async XLA Ops:
  174.1 203.9 %copy-start.3 = (s32[4]{0:T(128)S(1)}, s32[4]{0:T(128)}, u32[]{:S(2)}) copy-start(s32[4]{0:T(128)} %constant.46.clone) | copy-start | bytes 52
  278.4 37.0 %collective-permute-start.1 = (bf16[3,112,2304]{2,1,0:T(8,128)(2,1)}, bf16[3,112,2304]{2,1,0:T(8,128)(2,1)S(1)}, u32[]{:S(2)}, u32[]{:S(2)}) collective-permute-start(bf16[3,112,2304]{2,1,0:T(8,128)(2,1)} %gradients.3.refs_0_), channel_id=1, source_target_pairs={{0,6},{1,7},{2,0},{3,1},{4,2},{5,3},{6,4},{7,5},{8,14},{9,15},{10,... | collective-permute-start | bytes 4644872 | tf_op jit(solution)/shard_map/ppermute | solution.py:347
  280.4 68.3 %collective-permute-start.10 = (bf16[3,112,2304]{2,1,0:T(8,128)(2,1)}, bf16[3,112,2304]{2,1,0:T(8,128)(2,1)}, u32[]{:S(2)}, u32[]{:S(2)}) collective-permute-start(bf16[3,112,2304]{2,1,0:T(8,128)(2,1)} %get-tuple-element.30.refs_0_), channel_id=1, source_target_pairs={{0,6},{1,7},{2,0},{3,1},{4,2},{5,3},{6,4},{7,5},{8,14},{9,15},{10,... | collective-permute-start | bytes 4644872 | tf_op jit(solution)/shard_map/ppermute | solution.py:347
  280.5 72.6 %collective-permute-start.9 = (bf16[3,112,2304]{2,1,0:T(8,128)(2,1)}, bf16[3,112,2304]{2,1,0:T(8,128)(2,1)}, u32[]{:S(2)}, u32[]{:S(2)}) collective-permute-start(bf16[3,112,2304]{2,1,0:T(8,128)(2,1)} %get-tuple-element.30.refs_0_), channel_id=1, source_target_pairs={{0,2},{1,3},{2,4},{3,5},{4,6},{5,7},{6,0},{7,1},{8,10},{9,11},{10,... | collective-permute-start | bytes 4644872 | tf_op jit(solution)/shard_map/ppermute | solution.py:347
  282.4 71.9 %collective-permute-start = (bf16[3,112,2304]{2,1,0:T(8,128)(2,1)}, bf16[3,112,2304]{2,1,0:T(8,128)(2,1)S(1)}, u32[]{:S(2)}, u32[]{:S(2)}) collective-permute-start(bf16[3,112,2304]{2,1,0:T(8,128)(2,1)} %gradients.3.refs_0_), channel_id=1, source_target_pairs={{0,2},{1,3},{2,4},{3,5},{4,6},{5,7},{6,0},{7,1},{8,10},{9,11},{10,... | collective-permute-start | bytes 4644872 | tf_op jit(solution)/shard_map/ppermute | solution.py:347
  282.5 71.9 %collective-permute-start.13 = (bf16[3,112,2304]{2,1,0:T(8,128)(2,1)}, bf16[3,112,2304]{2,1,0:T(8,128)(2,1)}, u32[]{:S(2)}, u32[]{:S(2)}) collective-permute-start(bf16[3,112,2304]{2,1,0:T(8,128)(2,1)} %get-tuple-element.30.refs_0_), channel_id=1, source_target_pairs={{0,1},{1,0},{2,3},{3,2},{4,5},{5,4},{6,7},{7,6},{8,9},{9,8},{10,11... | collective-permute-start | bytes 4644872 | tf_op jit(solution)/shard_map/ppermute | solution.py:347
  315.4 95.4 %copy-start = (bf16[3,112,2304]{2,1,0:T(8,128)(2,1)}, bf16[3,112,2304]{2,1,0:T(8,128)(2,1)S(1)}, u32[]{:S(2)}) copy-start(bf16[3,112,2304]{2,1,0:T(8,128)(2,1)S(1)} %collective-permute-done.1.refs_2_) | copy-start | bytes 4644868
  315.5 49.8 %collective-permute-start.3 = (bf16[3,112,1152]{2,1,0:T(8,128)(2,1)S(1)}, bf16[3,112,1152]{2,1,0:T(8,128)(2,1)}, u32[]{:S(2)}, u32[]{:S(2)}) collective-permute-start(bf16[3,112,1152]{2,1,0:T(8,128)(2,1)S(1)} %slice.17), channel_id=1, source_target_pairs={{0,6},{1,7},{2,0},{3,1},{4,2},{5,3},{6,4},{7,5},{8,14},{9,15},{10,... | collective-permute-start | bytes 2322440 | tf_op jit(solution)/shard_map/ppermute | solution.py:347
  349.9 27.5 %collective-permute-start.12 = (bf16[3,112,1152]{2,1,0:T(8,128)(2,1)S(1)}, bf16[3,112,1152]{2,1,0:T(8,128)(2,1)}, u32[]{:S(2)}, u32[]{:S(2)}) collective-permute-start(bf16[3,112,1152]{2,1,0:T(8,128)(2,1)S(1)} %slice.19), channel_id=1, source_target_pairs={{0,6},{1,7},{2,0},{3,1},{4,2},{5,3},{6,4},{7,5},{8,14},{9,15},{10,... | collective-permute-start | bytes 2322440 | tf_op jit(solution)/shard_map/ppermute | solution.py:347
  353.1 39.4 %collective-permute-start.15 = (bf16[3,112,2304]{2,1,0:T(8,128)(2,1)}, bf16[3,112,2304]{2,1,0:T(8,128)(2,1)}, u32[]{:S(2)}, u32[]{:S(2)}) collective-permute-start(bf16[3,112,2304]{2,1,0:T(8,128)(2,1)} %collective-permute-done.10.refs_2_), channel_id=1, source_target_pairs={{0,1},{1,0},{2,3},{3,2},{4,5},{5,4},{6,7},{7,6},{8,9},{9,8},{10,11... | collective-permute-start | bytes 4644872 | tf_op jit(solution)/shard_map/ppermute | solution.py:347
  354.3 56.5 %copy-start.1 = (bf16[3,112,2304]{2,1,0:T(8,128)(2,1)}, bf16[3,112,2304]{2,1,0:T(8,128)(2,1)S(1)}, u32[]{:S(2)}) copy-start(bf16[3,112,2304]{2,1,0:T(8,128)(2,1)S(1)} %collective-permute-done.refs_1_) | copy-start | bytes 4644868
  354.4 23.0 %collective-permute-start.11 = (bf16[3,112,1152]{2,1,0:T(8,128)(2,1)S(1)}, bf16[3,112,1152]{2,1,0:T(8,128)(2,1)}, u32[]{:S(2)}, u32[]{:S(2)}) collective-permute-start(bf16[3,112,1152]{2,1,0:T(8,128)(2,1)S(1)} %slice.18), channel_id=1, source_target_pairs={{0,2},{1,3},{2,4},{3,5},{4,6},{5,7},{6,0},{7,1},{8,10},{9,11},{10,... | collective-permute-start | bytes 2322440 | tf_op jit(solution)/shard_map/ppermute | solution.py:347
  354.5 38.6 %collective-permute-start.14 = (bf16[3,112,2304]{2,1,0:T(8,128)(2,1)}, bf16[3,112,2304]{2,1,0:T(8,128)(2,1)}, u32[]{:S(2)}, u32[]{:S(2)}) collective-permute-start(bf16[3,112,2304]{2,1,0:T(8,128)(2,1)} %collective-permute-done.9.refs_1_), channel_id=1, source_target_pairs={{0,1},{1,0},{2,3},{3,2},{4,5},{5,4},{6,7},{7,6},{8,9},{9,8},{10,11... | collective-permute-start | bytes 4644872 | tf_op jit(solution)/shard_map/ppermute | solution.py:347
  365.3 26.7 %collective-permute-start.2 = (bf16[3,112,1152]{2,1,0:T(8,128)(2,1)}, bf16[3,112,1152]{2,1,0:T(8,128)(2,1)}, u32[]{:S(2)}, u32[]{:S(2)}) collective-permute-start(bf16[3,112,1152]{2,1,0:T(8,128)(2,1)} %slice.16), channel_id=1, source_target_pairs={{0,2},{1,3},{2,4},{3,5},{4,6},{5,7},{6,0},{7,1},{8,10},{9,11},{10,... | collective-permute-start | bytes 2322440 | tf_op jit(solution)/shard_map/ppermute | solution.py:347
  377.4 14.7 %collective-permute-start.17 = (bf16[3,112,1152]{2,1,0:T(8,128)(2,1)}, bf16[3,112,1152]{2,1,0:T(8,128)(2,1)}, u32[]{:S(2)}, u32[]{:S(2)}) collective-permute-start(bf16[3,112,1152]{2,1,0:T(8,128)(2,1)} %collective-permute-done.12.refs_4_), channel_id=1, source_target_pairs={{0,1},{1,0},{2,3},{3,2},{4,5},{5,4},{6,7},{7,6},{8,9},{9,8},{10,11... | collective-permute-start | bytes 2322440 | tf_op jit(solution)/shard_map/ppermute | solution.py:347
  377.4 15.3 %collective-permute-start.16 = (bf16[3,112,1152]{2,1,0:T(8,128)(2,1)}, bf16[3,112,1152]{2,1,0:T(8,128)(2,1)}, u32[]{:S(2)}, u32[]{:S(2)}) collective-permute-start(bf16[3,112,1152]{2,1,0:T(8,128)(2,1)} %collective-permute-done.11.refs_3_), channel_id=1, source_target_pairs={{0,1},{1,0},{2,3},{3,2},{4,5},{5,4},{6,7},{7,6},{8,9},{9,8},{10,11... | collective-permute-start | bytes 2322440 | tf_op jit(solution)/shard_map/ppermute | solution.py:347
  392.0 57.8 %collective-permute-start.4 = (bf16[3,112,2304]{2,1,0:T(8,128)(2,1)}, bf16[3,112,2304]{2,1,0:T(8,128)(2,1)}, u32[]{:S(2)}, u32[]{:S(2)}) collective-permute-start(bf16[3,112,2304]{2,1,0:T(8,128)(2,1)} %gradients.3.refs_0_), channel_id=1, source_target_pairs={{0,1},{1,0},{2,3},{3,2},{4,5},{5,4},{6,7},{7,6},{8,9},{9,8},{10,11... | collective-permute-start | bytes 4644872 | tf_op jit(solution)/shard_map/ppermute | solution.py:347
  392.0 57.8 %collective-permute-start.6 = (bf16[3,112,2304]{2,1,0:T(8,128)(2,1)S(1)}, bf16[3,112,2304]{2,1,0:T(8,128)(2,1)}, u32[]{:S(2)}, u32[]{:S(2)}) collective-permute-start(bf16[3,112,2304]{2,1,0:T(8,128)(2,1)S(1)} %collective-permute-done.1.refs_2_), channel_id=1, source_target_pairs={{0,1},{1,0},{2,3},{3,2},{4,5},{5,4},{6,7},{7,6},{8,9},{9,8},{10,11... | collective-permute-start | bytes 4644872 | tf_op jit(solution)/shard_map/ppermute | solution.py:347
  392.5 57.3 %collective-permute-start.5 = (bf16[3,112,2304]{2,1,0:T(8,128)(2,1)S(1)}, bf16[3,112,2304]{2,1,0:T(8,128)(2,1)}, u32[]{:S(2)}, u32[]{:S(2)}) collective-permute-start(bf16[3,112,2304]{2,1,0:T(8,128)(2,1)S(1)} %collective-permute-done.refs_1_), channel_id=1, source_target_pairs={{0,1},{1,0},{2,3},{3,2},{4,5},{5,4},{6,7},{7,6},{8,9},{9,8},{10,11... | collective-permute-start | bytes 4644872 | tf_op jit(solution)/shard_map/ppermute | solution.py:347
  392.6 57.2 %collective-permute-start.8 = (bf16[3,112,1152]{2,1,0:T(8,128)(2,1)}, bf16[3,112,1152]{2,1,0:T(8,128)(2,1)S(1)}, u32[]{:S(2)}, u32[]{:S(2)}) collective-permute-start(bf16[3,112,1152]{2,1,0:T(8,128)(2,1)} %collective-permute-done.3.refs_4_), channel_id=1, source_target_pairs={{0,1},{1,0},{2,3},{3,2},{4,5},{5,4},{6,7},{7,6},{8,9},{9,8},{10,11... | collective-permute-start | bytes 2322440 | tf_op jit(solution)/shard_map/ppermute | solution.py:347
  393.1 56.8 %collective-permute-start.7 = (bf16[3,112,1152]{2,1,0:T(8,128)(2,1)}, bf16[3,112,1152]{2,1,0:T(8,128)(2,1)}, u32[]{:S(2)}, u32[]{:S(2)}) collective-permute-start(bf16[3,112,1152]{2,1,0:T(8,128)(2,1)} %collective-permute-done.2.refs_3_), channel_id=1, source_target_pairs={{0,1},{1,0},{2,3},{3,2},{4,5},{5,4},{6,7},{7,6},{8,9},{9,8},{10,11... | collective-permute-start | bytes 2322440 | tf_op jit(solution)/shard_map/ppermute | solution.py:347
  449.8 0.9 copy-start.2
where the time goes:
time: 517 us; the launch traced here: 508 us
  Pallas kernels  391 us (76%)
  waiting for transfers between devices  96.9 us (19%)
  starting transfers between devices  13.6 us (3%)
    pallas_call x2, Pallas kernels, gradients(): pl.pallas_call(functools.partial(gradients_kernel, size, tile), name='gra...  212 us
    pallas_call x6, Pallas kernels, adamw(): pl.pallas_call(kernel, name='adamw', grid_spec=pltpu.PrefetchScalarGridSp...  113 us
    ppermute x18, waiting for transfers between devices, hop(): return lax.ppermute(one, 'dp', to)  96.9 us
    pallas_call x1, Pallas kernels, forward(): pl.pallas_call(functools.partial(forward_kernel, width), name='forward',...  36.6 us
    pallas_call x1, Pallas kernels, back(): pl.pallas_call(back_kernel, name='back', grid=(tokens // tile,), in_specs...  29.4 us
    ppermute x18, starting transfers between devices, hop(): return lax.ppermute(one, 'dp', to)  13.6 us
  transfers between devices with their start and end apart: 18, of which 5 were waited for; matrix products, arithmetic and copies ran while one was open for 1% of the time, Pallas kernels for 11%

commit v1 on v0

--- a/solution.py
+++ b/solution.py
@@ -41,17 +41,18 @@
     return [slice(i, i + width) for i in range(0, ff, width)]
 
 
-def forward_kernel(width, h_ref, wg_ref, wu_ref, wd_ref, o_ref, hid_ref):
+def forward_kernel(width, h_ref, wg_ref, wu_ref, wd_ref, o_ref, gate_ref, up_ref, hid_ref):
     wide = h_ref[...].astype(F32)
     a = normed(wide)
     for c in chunks(wg_ref.shape[1], width):
         gate, up = mm(a, wg_ref[:, c]), mm(a, wu_ref[:, c])
+        gate_ref[:, c], up_ref[:, c] = gate, up
         hid_ref[:, c] = (gate * sigmoid(gate) * up).astype(BF16)
     y = mm(hid_ref[...], wd_ref[...]).astype(BF16).astype(F32)
     o_ref[...] = (wide + y).astype(BF16)
 
 
-def forward(number, h, wg, wu, wd, tile=512, width=768):
+def forward(number, h, wg, wu, wd, tile=256, width=768):
     tokens, d = h.shape
     ff = wg.shape[2]
     return pl.pallas_call(
@@ -59,19 +60,22 @@
         name="forward",
         grid=(tokens // tile,),
         in_specs=[pl.BlockSpec((tile, d), lambda i: (i, 0)), layer_of(wg, number), layer_of(wu, number), layer_of(wd, number)],
-        out_specs=pl.BlockSpec((tile, d), lambda i: (i, 0)),
-        out_shape=jax.ShapeDtypeStruct((tokens, d), BF16),
+        out_specs=[pl.BlockSpec((tile, width), lambda i: (i, 0)) for width in (d, ff, ff)],
+        out_shape=[jax.ShapeDtypeStruct((tokens, d), BF16)] + [jax.ShapeDtypeStruct((tokens, ff), F32)] * 2,
         scratch_shapes=[pltpu.VMEM((tile, ff), BF16)],
         compiler_params=PARAMS(),
-        cost_estimate=cost(6 * tokens * d * ff, 2 * (2 * tokens * d + 3 * d * ff)),
+        cost_estimate=cost(6 * tokens * d * ff, 2 * (2 * tokens * d + 3 * d * ff + 4 * tokens * ff)),
     )(h, wg, wu, wd)
 
 
-PAIRED, PASSED, ARRIVED = 2, 4, 6
-
-
-def gradients_kernel(size, tile, h_ref, dy_ref, wg_ref, wu_ref, wd_ref, o_ref, *refs):
-    *kept, a, x, y, g, pr, p, r1a, r1b, r2a, r2b, send, recv = refs
+PAIRED, PASSED, ARRIVED = 3, 6, 9
+
+
+def gradients_kernel(size, tile, known, h_ref, dy_ref, gate_ref, up_ref, wd_ref, o_ref, *refs):
+    *kept, x, y, g, pr, p, r1a, r1b, r2a, r2b, send, recv = refs
+    tokens = h_ref.shape[0]
+    if not known:
+        *kept, a = kept
     step = pl.program_id(0)
     steps = pl.num_programs(0) - ARRIVED // 3
     pieces = 3 * steps
@@ -117,17 +121,18 @@
         for device in (partner, left, right):
             pl.semaphore_signal(barrier, inc=1, device_id={"dp": device}, device_id_type=pl.DeviceIdType.MESH)
         pl.semaphore_wait(barrier, 3)
-        for i in range(0, a.shape[0], tile):
+        for i in range(0, tokens, tile):
             part = normed(h_ref[i : i + tile].astype(F32))
-            a[i : i + tile] = part
+            if not known:
+                a[i : i + tile] = part
             x[0, :, i : i + tile] = dy_ref[i : i + tile].T
             x[1, :, i : i + tile] = part.T
 
     @pl.when(step < steps)
     def _():
-        for i in range(0, a.shape[0], tile):
+        for i in range(0, tokens, tile):
             t = slice(i, i + tile)
-            gate, up = mm(a[t], wg_ref[...]), mm(a[t], wu_ref[...])
+            gate, up = (gate_ref[t], up_ref[t]) if known else (mm(a[t], gate_ref[...]), mm(a[t], up_ref[...]))
             by_hid = mm(dy_ref[t], wd_ref[...], 1, 1).astype(BF16).astype(F32)
             s = sigmoid(gate)
             silu = gate * s
@@ -171,7 +176,7 @@
             for one in second(j):
                 one.wait()
             total = (p[j, of_chip(0)].astype(F32) + r2a[j].astype(F32) + r2b[j].astype(F32)).astype(BF16)
-            o_ref[lax.rem(j, 3), :, pl.ds(pl.multiple_of((j // 3) * width, 128), width)] = total
+            o_ref[lax.rem(j + 2, 3), :, pl.ds(pl.multiple_of((j // 3) * width, 128), width)] = total
 
         @stage(PASSED)
         def _():
@@ -188,7 +193,7 @@
             to_partner(k).start()
 
 
-def gradients(size, number, h, dy, wg, wu, wd, keep, width=256, tile=512):
+def gradients(size, number, h, dy, known, wg, wu, wd, keep, width=256, tile=512):
     tokens, d = h.shape
     ff = wg.shape[2]
     steps, rows, half = ff // width, d // size, d // 2
@@ -197,20 +202,23 @@
     def now(k):
         return jnp.minimum(k, steps - 1)
 
-    column = pl.BlockSpec((None, d, width), lambda k: (number, 0, now(k)))
+    if known:
+        column, pair = pl.BlockSpec((tokens, width), lambda k: (0, now(k))), known
+    else:
+        column, pair = pl.BlockSpec((None, d, width), lambda k: (number, 0, now(k))), (wg, wu)
     out_specs, out_shape = [whole((3, rows, ff))], [jax.ShapeDtypeStruct((3, rows, ff), BF16)]
     if keep:
         out_specs += [pl.BlockSpec((2, tokens, width), lambda k: (0, 0, now(k)))]
         out_shape += [jax.ShapeDtypeStruct((2, tokens, ff), BF16)]
     return pl.pallas_call(
-        functools.partial(gradients_kernel, size, tile),
+        functools.partial(gradients_kernel, size, tile, bool(known)),
         name="gradients",
         grid=(steps + ARRIVED // 3,),
         in_specs=[whole((tokens, d))] * 2 + [column, column, pl.BlockSpec((None, width, d), lambda k: (number, now(k), 0))],
         out_specs=out_specs,
         out_shape=out_shape,
         scratch_shapes=[
-            pltpu.VMEM((tokens, d), BF16),
+            *([] if known else [pltpu.VMEM((tokens, d), BF16)]),
             pltpu.VMEM((2, d, tokens), BF16),
             pltpu.VMEM((3, tokens, width), BF16),
             pltpu.VMEM((PAIRED + 1, d, width), BF16),
@@ -224,8 +232,8 @@
             pltpu.SemaphoreType.DMA((5, pieces)),
         ],
         compiler_params=PARAMS(collective_id=number, has_side_effects=True),
-        cost_estimate=cost(18 * tokens * d * ff, 2 * (2 * tokens * d + 2 * tokens * ff + 6 * d * ff)),
-    )(h, dy, wg, wu, wd)
+        cost_estimate=cost((8 if known else 12) * tokens * d * ff, 2 * (2 * tokens * d + 2 * tokens * ff + 6 * d * ff)),
+    )(h, dy, *pair, wd)
 
 
 def back_kernel(h_ref, dy_ref, dg_ref, du_ref, wg_ref, wu_ref, o_ref):
@@ -254,78 +262,129 @@
     )(h, dy, y, y, wg, wu)
 
 
-def adamw_step(g, w_ref, m_ref, v_ref, ow_ref, om_ref, ov_ref):
-    g = g.astype(F32)
-    m = 0.9 * m_ref[...] + 0.1 * g
-    v = 0.95 * v_ref[...] + 0.05 * g * g
-    w = w_ref[...].astype(F32)
-    ow_ref[...] = (w - 0.02 * (m * lax.rsqrt(v + 1e-8) + 0.1 * w)).astype(BF16)
-    om_ref[...] = m
-    ov_ref[...] = v
-
-
-def adamw_kernel(place_ref, w_ref, m_ref, v_ref, *refs):
-    parts, outs = refs[:10], refs[-3:]
-    for which in range(8):
-
-        @pl.when(pl.program_id(0) == which)
-        def _(which=which):
-            group = parts[5 * (which // 4) :]
-            at = which % 4
-            g = group[at][...] if at < 3 else jnp.concatenate([group[3][...], group[4][...]], 1)
-            adamw_step(g, w_ref, m_ref, v_ref, *outs)
-
-
-def adamw_turned_kernel(place_ref, w_ref, m_ref, v_ref, *refs):
-    parts, outs, g_ref = refs[:10], refs[-4:-1], refs[-1]
-    rows = parts[0].shape[0]
-    early = pl.program_id(0) < pl.num_programs(0) // 2
-
-    def put(which, value):
-        g_ref[pl.ds(pl.multiple_of(place_ref[which] * rows, 16), rows)] = value
-
-    for which in range(8):
-        group = parts[5 * (which // 4) :]
-        at = which % 4
+FLIGHT = 3
+
+
+def adamw_kernel(number, first, count, blocks, size, turned, aliased, *refs):
+    parts, refs = refs[:10], refs[10:]
+    sources, refs = refs[: 3 * count], refs[3 * count + aliased :]
+    targets, refs = refs[: 3 * count], refs[3 * count :]
+    g_buf, wi, mi, vi, wo, mo, vo, g_sem, in_sem, out_sem = refs
+    rows, per = wi.shape[1], blocks // count
+    shard, middle = parts[0].shape[1], parts[3].shape[2]
+    quarters = size // 2
+    me = lax.axis_index("dp")
+    core, chip = lax.rem(me, 2), me // 2
+
+    def place(which):
+        at = lax.rem(which, 4)
+        offset = jnp.where(at == 1, quarters - 1, jnp.where(at == 2, 1, jnp.where(at == 3, 2, 0)))
+        side = jnp.where(which < 4, core, 1 - core)
+        return side * quarters + lax.rem(chip + offset, quarters)
+
+    def of_shard(which, matrix, target, sem):
+        group, at = parts[5 * (which // 4) :], which % 4
         if at < 3:
-            put(which, group[at][...])
-        else:
-            put(which, jnp.where(early, group[3][...], group[4][...]))
-    adamw_step(g_ref[...].T, w_ref, m_ref, v_ref, *outs)
-
-
-def adamw(place, number, at, parts, w, m, v, turned, so_far, width=384):
-    rows, ff = parts[0].shape[1:]
-    d = rows * place.shape[0]
+            return [pltpu.make_async_copy(group[at].at[matrix], target, sem)]
+        return [
+            pltpu.make_async_copy(group[3].at[matrix], target.at[:, pl.ds(0, middle)], sem),
+            pltpu.make_async_copy(group[4].at[matrix], target.at[:, pl.ds(middle, middle)], sem),
+        ]
+
+    def move(c, arrays, buffers, sem, into):
+        slot, block = lax.rem(c, FLIGHT), lax.rem(c, per)
+        start = block if turned else place(block)
+        here = pl.ds(pl.multiple_of(start * rows, 16), rows)
+        for matrix in range(count):
+
+            @pl.when(c // per == matrix)
+            def _(matrix=matrix):
+                for kind in range(3):
+                    far, near = arrays[kind * count + matrix].at[number, here], buffers[kind].at[slot]
+                    pltpu.make_async_copy(*((far, near) if into else (near, far)), sem.at[kind, slot]).start()
+
+                if into and not turned:
+                    for which in range(8):
+
+                        @pl.when(block == which)
+                        def _(which=which):
+                            for one in of_shard(which, first + matrix, g_buf.at[slot], g_sem.at[slot]):
+                                one.start()
+
+    def settle(c, arrays, buffers, sem, into):
+        slot = lax.rem(c, FLIGHT)
+        for kind in range(3):
+            far, near = arrays[kind * count].at[number, pl.ds(0, rows)], buffers[kind].at[slot]
+            pltpu.make_async_copy(*((far, near) if into else (near, far)), sem.at[kind, slot]).wait()
+        if into and not turned:
+            pltpu.make_async_copy(parts[0].at[first], g_buf.at[slot], g_sem.at[slot]).wait()
+
+    def fetch(c):
+        move(c, sources, (wi, mi, vi), in_sem, True)
+
+    if turned:
+        for which in range(8):
+            for one in of_shard(which, first, g_buf.at[pl.ds(pl.multiple_of(place(which) * shard, 16), shard)], g_sem.at[which]):
+                one.start()
+    for c in range(FLIGHT):
+        fetch(c)
+    if turned:
+        for which in range(8):
+            pltpu.make_async_copy(parts[0].at[first], g_buf.at[pl.ds(0, shard)], g_sem.at[which]).wait()
+
+    @pl.loop(0, blocks)
+    def _(c):
+        slot = lax.rem(c, FLIGHT)
+        settle(c, sources, (wi, mi, vi), in_sem, True)
+
+        @pl.when(c >= FLIGHT)
+        def _():
+            settle(c - FLIGHT, targets, (wo, mo, vo), out_sem, False)
+
+        g = g_buf[:, pl.ds(pl.multiple_of(c * rows, 128), rows)].T if turned else g_buf[slot]
+        g = g.astype(F32)
+        m = 0.9 * mi[slot] + 0.1 * g
+        v = 0.95 * vi[slot] + 0.05 * g * g
+        w = wi[slot].astype(F32)
+        wo[slot] = (w - 0.02 * (m * lax.rsqrt(v + 1e-8) + 0.1 * w)).astype(BF16)
+        mo[slot] = m
+        vo[slot] = v
+        move(c, targets, (wo, mo, vo), out_sem, False)
+
+        @pl.when(c + FLIGHT < blocks)
+        def _():
+            fetch(c + FLIGHT)
+
+    for c in range(blocks - FLIGHT, blocks):
+        settle(c, targets, (wo, mo, vo), out_sem, False)
+
+
+def adamw(size, number, first, parts, weights, moments, squares, turned, so_far, width=256):
+    count = len(weights)
+    shard, ff = parts[0].shape[1:]
+    d = shard * size
     so_far = so_far or ()
-    if turned:
-        steps, kernel = ff // width, adamw_turned_kernel
-        per = steps // 2
-        big = pl.BlockSpec((None, width, d), lambda i, place: (number, i, 0))
-        three = [pl.BlockSpec((None, rows, width), lambda i, place: (at, 0, i))] * 3
-        three += [pl.BlockSpec((None, rows, width), lambda i, place: (at, 0, jnp.minimum(i, per - 1)))]
-        three += [pl.BlockSpec((None, rows, width), lambda i, place: (at, 0, jnp.maximum(i - per, 0)))]
-        scratch = [pltpu.VMEM((d, width), BF16)]
-    else:
-        steps, kernel = place.shape[0], adamw_kernel
-        big = pl.BlockSpec((None, rows, ff), lambda i, place: (number, place[i], 0))
-        three = [pl.BlockSpec((None, *part.shape[1:]), lambda i, place: (at, 0, 0), pipeline_mode=pl.Buffered(1)) for part in parts[:5]]
-        scratch = []
+    rows, columns = (width, d) if turned else (shard, ff)
+    blocks = count * weights[0].shape[1] // rows
+    hbm = pl.BlockSpec(memory_space=pl.ANY)
+    inputs = (*parts, *weights, *moments, *squares, *so_far)
     return pl.pallas_call(
-        kernel,
+        functools.partial(adamw_kernel, number, first, count, blocks, size, turned, len(so_far)),
         name="adamw",
-        grid_spec=pltpu.PrefetchScalarGridSpec(
-            num_scalar_prefetch=1,
-            grid=(steps,),
-            in_specs=[big, big, big, *three, *three, *[pl.BlockSpec(memory_space=pl.ANY)] * len(so_far)],
-            out_specs=[big] * 3,
-            scratch_shapes=scratch,
-        ),
-        out_shape=[jax.ShapeDtypeStruct(w.shape, BF16), jax.ShapeDtypeStruct(m.shape, F32), jax.ShapeDtypeStruct(v.shape, F32)],
-        input_output_aliases={14 + i: i for i in range(len(so_far))},
+        in_specs=[hbm] * len(inputs),
+        out_specs=[hbm] * (3 * count),
+        out_shape=[jax.ShapeDtypeStruct(one.shape, one.dtype) for one in (*weights, *moments, *squares)],
+        scratch_shapes=[
+            pltpu.VMEM((d, ff) if turned else (FLIGHT, rows, columns), BF16),
+            *[pltpu.VMEM((FLIGHT, rows, columns), dtype) for dtype in (BF16, F32, F32) * 2],
+            pltpu.SemaphoreType.DMA((8,) if turned else (FLIGHT,)),
+            pltpu.SemaphoreType.DMA((3, FLIGHT)),
+            pltpu.SemaphoreType.DMA((3, FLIGHT)),
+        ],
+        input_output_aliases={10 + 3 * count + i: i for i in range(len(so_far))},
         compiler_params=PARAMS(),
-        cost_estimate=cost(5 * 2048 * d * ff // 2, 22 * d * ff),
-    )(place, w, m, v, *parts, *so_far)
+        cost_estimate=cost(count * 5 * 2048 * d * ff // 2, count * 22 * d * ff),
+    )(*inputs)
 
 
 def solution(mesh):
@@ -337,11 +396,6 @@
     def step(x, dy, *arrays):
         weights, moments, squares = (arrays[i : i + 3] for i in (0, 3, 6))
         layers = weights[0].shape[0]
-        me = lax.axis_index("dp")
-        core, chip = me % 2, me // 2
-        offsets = jnp.array([0, size // 2 - 1, 1, 2], jnp.int32)
-        place = ((chip + offsets) % (size // 2))[None] + jnp.stack([core, 1 - core])[:, None] * (size // 2)
-        place = place.reshape(-1).astype(jnp.int32)
 
         def hop(one, to):
             return lax.ppermute(one, "dp", to)
@@ -355,22 +409,24 @@
             pairs += [hop(first, swap), hop(second, swap)]
             return (own, left, right, first, second, *pairs)
 
-        h, kept = x[0], []
+        h, kept, known = x[0], [], []
         for number in range(layers):
             kept.append(h)
+            both = ()
             if number < layers - 1:
-                h = forward(number, h, *weights)
-        by_h, out, sums = dy[0], [None] * 3, []
+                h, *both = forward(number, h, *weights)
+            known.append(both)
+        by_h, every = dy[0], []
         for number in reversed(range(layers)):
-            own, *by_both = gradients(size, number, kept[number], by_h, *weights, number > 0)
-            parts = gathered(own)
-            for at, which in enumerate((2, 0, 1)):
-                sums.append((number, which, at, parts))
+            own, *by_both = gradients(size, number, kept[number], by_h, known[number], *weights, number > 0)
+            every.append((number, gathered(own)))
             if number:
                 by_h = back(number, kept[number], by_h, by_both[0], *weights[:2])
-        for number, which, at, parts in sums:
-            out[which] = adamw(place, number, at, parts, weights[which], moments[which], squares[which], which == 2, out[which])
-        return tuple(one[which] for which in range(3) for one in out)
+        side, down = None, None
+        for number, parts in every:
+            side = adamw(size, number, 0, parts, weights[:2], moments[:2], squares[:2], False, side)
+            down = adamw(size, number, 2, parts, weights[2:], moments[2:], squares[2:], True, down)
+        return tuple(one for kind in range(3) for one in (*side[2 * kind : 2 * kind + 2], down[kind]))
 
     return jax.shard_map(
         step,

time: 517 us -> 457 us (0.88); the launches traced: 508 us -> 457 us
  Pallas kernels: 391 us -> 344 us
    pallas_call x8 -> x6, Pallas kernels: 325 us -> 277 us  [the longest x2 181 us: gradients(): pl.pallas_call(functools.partial(gradients_kernel, size, tile, bool(known...]
  transfers between devices with their start and end apart: 18 -> 18, of which waited for: 5 -> 5; matrix products, arithmetic and copies ran while one was open for 1% -> 0% of each run, Pallas kernels for 11% -> 11%
where the time goes in v1:
time: 457 us
  Pallas kernels  344 us (75%)
  waiting for transfers between devices  97.8 us (21%)
  starting transfers between devices  12.2 us (3%)
    pallas_call x2, Pallas kernels, gradients(): pl.pallas_call(functools.partial(gradients_kernel, size, tile, bool(known...  181 us
    ppermute x18, waiting for transfers between devices, hop(): return lax.ppermute(one, 'dp', to)  97.8 us
    pallas_call x4, Pallas kernels, adamw(): pl.pallas_call(functools.partial(adamw_kernel, number, first, count, bloc...  96.4 us
    pallas_call x1, Pallas kernels, forward(): pl.pallas_call(functools.partial(forward_kernel, width), name='forward',...  37.4 us
    pallas_call x1, Pallas kernels, back(): pl.pallas_call(back_kernel, name='back', grid=(tokens // tile,), in_specs...  29.7 us
    ppermute x18, starting transfers between devices, hop(): return lax.ppermute(one, 'dp', to)  12.2 us
  transfers between devices with their start and end apart: 18, of which 5 were waited for; matrix products, arithmetic and copies ran while one was open for 0% of the time, Pallas kernels for 11%

profile of v1, /device:TPU:112, one launch (start us, length us, event | category | flops | bytes accessed | tf_op | source)
XLA Modules:
  0.0 457.1 jit_solution(1672874754473448899)
XLA Ops:
  0.6 37.4 %forward.1 = (bf16[2048,896]{1,0:T(8,128)(2,1)}, f32[2048,2304]{1,0:T(8,128)}, f32[2048,2304]{1,0:T(8,128)}) custom-call(bf16[2048,896]{1,0:T(8,128)(2,1)} %bitcast.4, bf16[2,896,2304]{2,1,0:T(8,128)(2,1)} %refs_10_.5, bf16[2,896,2304]{2,1,0:T(8,128)(2,1)} %refs_11_.5, bf16[2,2304,896]{2,1,0:T(8,128)(2,1)} %refs_10_.7), custom_call_target="tpu_custom_call" | custom-call | flops 25367150592 | bytes 57475072 | tf_op jit(solution)/shard_map/forward/pallas_call | solution.py:58
  38.0 98.5 %gradients.2 = (bf16[3,112,2304]{2,1,0:T(8,128)(2,1)}, bf16[2,2048,2304]{2,1,0:T(8,128)(2,1)}) custom-call(bf16[2048,896]{1,0:T(8,128)(2,1)} %get-tuple-element.32.h_ref, bf16[2048,896]{1,0:T(8,128)(2,1)} %bitcast.2, bf16[2,896,2304]{2,1,0:T(8,128)(2,1)} %refs_10_.5, bf16[2,896,2304]{2,1,0:T(8,128)(2,1)} %refs_11_.5, bf16[2,2304,896]{2,1,0:T(8,128)(2,1)} %refs_10_.7), custom_call_target="tpu_custom_call" | custom-call | flops 50734301184 | bytes 50987008 | tf_op jit(solution)/shard_map/gradients/pallas_call | solution.py:213
  136.5 29.7 %back.1.dy_ref = bf16[2048,896]{1,0:T(8,128)(2,1)} custom-call(bf16[2048,896]{1,0:T(8,128)(2,1)} %get-tuple-element.32.h_ref, bf16[2048,896]{1,0:T(8,128)(2,1)} %bitcast.3, bf16[2,2048,2304]{2,1,0:T(8,128)(2,1)} %get-tuple-element.33.dg_ref.du_ref, bf16[2,2048,2304]{2,1,0:T(8,128)(2,1)} %get-tuple-element.33.dg_ref.du_ref, bf16[2,896,2304]{2,1,0:T(8,128)(2,1)} %refs_10_.5, ...), custom_call_target="tpu_custom_call" | custom-call | flops 16911433728 | bytes 38141952 | tf_op jit(solution)/shard_map/back/pallas_call | solution.py:253
  166.2 82.3 %gradients.3.refs_0_ = bf16[3,112,2304]{2,1,0:T(8,128)(2,1)} custom-call(bf16[2048,896]{1,0:T(8,128)(2,1)} %bitcast.5, bf16[2048,896]{1,0:T(8,128)(2,1)} %back.1.dy_ref, f32[2048,2304]{1,0:T(8,128)} %get-tuple-element.34.gate_ref, f32[2048,2304]{1,0:T(8,128)} %get-tuple-element.35.up_ref, bf16[2,2304,896]{2,1,0:T(8,128)(2,1)} %refs_10_.7), custom_call_target="tpu_custom_call" | custom-call | flops 33822867456 | bytes 50987008 | tf_op jit(solution)/shard_map/gradients/pallas_call | solution.py:213
  248.5 0.8 collective-permute-start
  249.2 0.7 collective-permute-start.9
  250.0 2.5 collective-permute-start.10
  252.5 1.3 collective-permute-start.1
  253.8 32.9 %collective-permute-done.refs_1_ = bf16[3,112,2304]{2,1,0:T(8,128)(2,1)S(1)} collective-permute-done((bf16[3,112,2304]{2,1,0:T(8,128)(2,1)}, bf16[3,112,2304]{2,1,0:T(8,128)(2,1)S(1)}, u32[]{:S(2)}, u32[]{:S(2)}) %collective-permute-start) | collective-permute-done | bytes 1548320 | tf_op jit(solution)/shard_map/ppermute | solution.py:401
  286.7 0.1 slice.16
  286.8 0.1 collective-permute-start.2
  286.9 33.0 %collective-permute-done.9.refs_1_ = bf16[3,112,2304]{2,1,0:T(8,128)(2,1)S(1)} collective-permute-done((bf16[3,112,2304]{2,1,0:T(8,128)(2,1)}, bf16[3,112,2304]{2,1,0:T(8,128)(2,1)S(1)}, u32[]{:S(2)}, u32[]{:S(2)}) %collective-permute-start.9) | collective-permute-done | bytes 1548320 | tf_op jit(solution)/shard_map/ppermute | solution.py:401
  320.0 0.1 collective-permute-start.14
  320.1 0.1 slice.19
  320.1 0.5 collective-permute-start.15
  320.7 3.2 collective-permute-start.12
  324.0 12.5 %collective-permute-done.2.refs_3_ = bf16[3,112,1152]{2,1,0:T(8,128)(2,1)S(1)} collective-permute-done((bf16[3,112,1152]{2,1,0:T(8,128)(2,1)S(1)}, bf16[3,112,1152]{2,1,0:T(8,128)(2,1)S(1)}, u32[]{:S(2)}, u32[]{:S(2)}) %collective-permute-start.2) | collective-permute-done | bytes 774176 | tf_op jit(solution)/shard_map/ppermute | solution.py:401
  336.5 0.7 collective-permute-start.3
  337.2 12.8 %collective-permute-done.11.refs_3_ = bf16[3,112,1152]{2,1,0:T(8,128)(2,1)S(1)} collective-permute-done((bf16[3,112,1152]{2,1,0:T(8,128)(2,1)S(1)}, bf16[3,112,1152]{2,1,0:T(8,128)(2,1)S(1)}, u32[]{:S(2)}, u32[]{:S(2)}) %collective-permute-start.11) | collective-permute-done | bytes 774176 | tf_op jit(solution)/shard_map/ppermute | solution.py:401
  350.0 0.5 collective-permute-start.17
  350.5 6.5 %collective-permute-done.3.refs_4_ = bf16[3,112,1152]{2,1,0:T(8,128)(2,1)} collective-permute-done((bf16[3,112,1152]{2,1,0:T(8,128)(2,1)S(1)}, bf16[3,112,1152]{2,1,0:T(8,128)(2,1)}, u32[]{:S(2)}, u32[]{:S(2)}) %collective-permute-start.3) | collective-permute-done | bytes 774176 | tf_op jit(solution)/shard_map/ppermute | solution.py:401
  357.1 0.5 collective-permute-start.5
  357.6 0.1 collective-permute-start.6
  357.7 0.5 copy-done.5
  358.2 0.5 collective-permute-start.7
  358.8 0.3 copy-done.10
  359.1 0.9 copy-done.11
  360.0 0.5 collective-permute-start.8
  360.5 30.9 %adamw.4 = (bf16[2,896,2304]{2,1,0:T(8,128)(2,1)}, bf16[2,896,2304]{2,1,0:T(8,128)(2,1)}, f32[2,896,2304]{2,1,0:T(8,128)}, f32[2,896,2304]{2,1,0:T(8,128)}, f32[...) custom-call(bf16[3,112,2304]{2,1,0:T(8,128)(2,1)} %get-tuple-element.36.refs_0_, bf16[3,112,2304]{2,1,0:T(8,128)(2,1)} %copy-done.2, ...), custom_call_target="tpu_custom_call" | custom-call | flops 21139292160 | bytes 90832896 | tf_op jit(solution)/shard_map/adamw/pallas_call | solution.py:371
  391.4 17.3 %adamw.6 = (bf16[2,2304,896]{2,1,0:T(8,128)(2,1)}, f32[2,2304,896]{2,1,0:T(8,128)}, f32[2,2304,896]{2,1,0:T(8,128)}) custom-call(bf16[3,112,2304]{2,1,0:T(8,128)(2,1)} %get-tuple-element.36.refs_0_, bf16[3,112,2304]{2,1,0:T(8,128)(2,1)} %copy-done.2, bf16[3,112,2304]{2,1,0:T(8,128)(2,1)} %copy-done.3, bf16[3,112,1152]{2,1,0:T(8,128)(2,1)} %copy-done.8, ...), custom_call_target="tpu_custom_call" | custom-call | flops 10569646080 | bytes 45416448 | tf_op jit(solution)/shard_map/adamw/pallas_call | solution.py:371
  408.7 17.3 %adamw.7 = (bf16[2,2304,896]{2,1,0:T(8,128)(2,1)}, f32[2,2304,896]{2,1,0:T(8,128)}, f32[2,2304,896]{2,1,0:T(8,128)}) custom-call(bf16[3,112,2304]{2,1,0:T(8,128)(2,1)} %gradients.3.refs_0_, bf16[3,112,2304]{2,1,0:T(8,128)(2,1)} %copy-done, bf16[3,112,2304]{2,1,0:T(8,128)(2,1)} %copy-done.1, ...), custom_call_target="tpu_custom_call", output_to_operand_aliasing={{0}: (13, {}), {1}: (14, {}), {2}: (15, {})} | custom-call | flops 10569646080 | bytes 45416448 | tf_op jit(solution)/shard_map/adamw/pallas_call | solution.py:371
  426.1 30.8 %adamw.5 = (bf16[2,896,2304]{2,1,0:T(8,128)(2,1)}, bf16[2,896,2304]{2,1,0:T(8,128)(2,1)}, f32[2,896,2304]{2,1,0:T(8,128)}, f32[2,896,2304]{2,1,0:T(8,128)}, f32[...) custom-call(bf16[3,112,2304]{2,1,0:T(8,128)(2,1)} %gradients.3.refs_, ...), custom_call_target="tpu_custom_call", output_to_operand_aliasing={{0}: (16, {}), {1}: (17, {}), {2}: (18, {}), {3}: (19, {}),... | custom-call | flops 21139292160 | bytes 90832896 | tf_op jit(solution)/shard_map/adamw/pallas_call | solution.py:371
  (40 shorter events, 0.3 us)
Async XLA Ops:
  248.5 38.2 %collective-permute-start = (bf16[3,112,2304]{2,1,0:T(8,128)(2,1)}, bf16[3,112,2304]{2,1,0:T(8,128)(2,1)S(1)}, u32[]{:S(2)}, u32[]{:S(2)}) collective-permute-start(bf16[3,112,2304]{2,1,0:T(8,128)(2,1)} %gradients.3.refs_0_), channel_id=1, source_target_pairs={{0,2},{1,3},{2,4},{3,5},{4,6},{5,7},{6,0},{7,1},{8,10},{9,11},{10,... | collective-permute-start | bytes 4644872 | tf_op jit(solution)/shard_map/ppermute | solution.py:401
  249.2 70.6 %collective-permute-start.9 = (bf16[3,112,2304]{2,1,0:T(8,128)(2,1)}, bf16[3,112,2304]{2,1,0:T(8,128)(2,1)S(1)}, u32[]{:S(2)}, u32[]{:S(2)}) collective-permute-start(bf16[3,112,2304]{2,1,0:T(8,128)(2,1)} %get-tuple-element.36.refs_0_), channel_id=1, source_target_pairs={{0,2},{1,3},{2,4},{3,5},{4,6},{5,7},{6,0},{7,1},{8,10},{9,11},{10,... | collective-permute-start | bytes 4644872 | tf_op jit(solution)/shard_map/ppermute | solution.py:401
  250.0 70.1 %collective-permute-start.10 = (bf16[3,112,2304]{2,1,0:T(8,128)(2,1)}, bf16[3,112,2304]{2,1,0:T(8,128)(2,1)S(1)}, u32[]{:S(2)}, u32[]{:S(2)}) collective-permute-start(bf16[3,112,2304]{2,1,0:T(8,128)(2,1)} %get-tuple-element.36.refs_0_), channel_id=1, source_target_pairs={{0,6},{1,7},{2,0},{3,1},{4,2},{5,3},{6,4},{7,5},{8,14},{9,15},{10,... | collective-permute-start | bytes 4644872 | tf_op jit(solution)/shard_map/ppermute | solution.py:401
  252.5 68.2 %collective-permute-start.1 = (bf16[3,112,2304]{2,1,0:T(8,128)(2,1)}, bf16[3,112,2304]{2,1,0:T(8,128)(2,1)S(1)}, u32[]{:S(2)}, u32[]{:S(2)}) collective-permute-start(bf16[3,112,2304]{2,1,0:T(8,128)(2,1)} %gradients.3.refs_0_), channel_id=1, source_target_pairs={{0,6},{1,7},{2,0},{3,1},{4,2},{5,3},{6,4},{7,5},{8,14},{9,15},{10,... | collective-permute-start | bytes 4644872 | tf_op jit(solution)/shard_map/ppermute | solution.py:401
  253.8 66.9 %collective-permute-start.13 = (bf16[3,112,2304]{2,1,0:T(8,128)(2,1)}, bf16[3,112,2304]{2,1,0:T(8,128)(2,1)S(1)}, u32[]{:S(2)}, u32[]{:S(2)}) collective-permute-start(bf16[3,112,2304]{2,1,0:T(8,128)(2,1)} %get-tuple-element.36.refs_0_), channel_id=1, source_target_pairs={{0,1},{1,0},{2,3},{3,2},{4,5},{5,4},{6,7},{7,6},{8,9},{9,8},{10,11... | collective-permute-start | bytes 4644872 | tf_op jit(solution)/shard_map/ppermute | solution.py:401
  286.7 104.6 %copy-start = (bf16[3,112,2304]{2,1,0:T(8,128)(2,1)}, bf16[3,112,2304]{2,1,0:T(8,128)(2,1)S(1)}, u32[]{:S(2)}) copy-start(bf16[3,112,2304]{2,1,0:T(8,128)(2,1)S(1)} %collective-permute-done.refs_1_) | copy-start | bytes 4644868
  286.8 49.7 %collective-permute-start.2 = (bf16[3,112,1152]{2,1,0:T(8,128)(2,1)S(1)}, bf16[3,112,1152]{2,1,0:T(8,128)(2,1)S(1)}, u32[]{:S(2)}, u32[]{:S(2)}) collective-permute-start(bf16[3,112,1152]{2,1,0:T(8,128)(2,1)S(1)} %slice.16), channel_id=1, source_target_pairs={{0,2},{1,3},{2,4},{3,5},{4,6},{5,7},{6,0},{7,1},{8,10},{9,11},{10,... | collective-permute-start | bytes 2322440 | tf_op jit(solution)/shard_map/ppermute | solution.py:401
  319.9 37.7 %copy-start.2 = (bf16[3,112,2304]{2,1,0:T(8,128)(2,1)}, bf16[3,112,2304]{2,1,0:T(8,128)(2,1)S(1)}, u32[]{:S(2)}) copy-start(bf16[3,112,2304]{2,1,0:T(8,128)(2,1)S(1)} %collective-permute-done.9.refs_1_) | copy-start | bytes 4644868
  320.0 37.1 %collective-permute-start.14 = (bf16[3,112,2304]{2,1,0:T(8,128)(2,1)S(1)}, bf16[3,112,2304]{2,1,0:T(8,128)(2,1)S(1)}, u32[]{:S(2)}, u32[]{:S(2)}) collective-permute-start(bf16[3,112,2304]{2,1,0:T(8,128)(2,1)S(1)} %collective-permute-done.9.refs_1_), channel_id=1, source_target_pairs={{0,1},{1,0},{2,3},{3,2},{4,5},{5,4},{6,7},{7,6},{8,9},{9,8},{10,11... | collective-permute-start | bytes 4644872 | tf_op jit(solution)/shard_map/ppermute | solution.py:401
  320.1 37.5 %copy-start.3 = (bf16[3,112,2304]{2,1,0:T(8,128)(2,1)}, bf16[3,112,2304]{2,1,0:T(8,128)(2,1)S(1)}, u32[]{:S(2)}) copy-start(bf16[3,112,2304]{2,1,0:T(8,128)(2,1)S(1)} %collective-permute-done.10.refs_2_) | copy-start | bytes 4644868
  320.1 37.4 %collective-permute-start.15 = (bf16[3,112,2304]{2,1,0:T(8,128)(2,1)S(1)}, bf16[3,112,2304]{2,1,0:T(8,128)(2,1)S(1)}, u32[]{:S(2)}, u32[]{:S(2)}) collective-permute-start(bf16[3,112,2304]{2,1,0:T(8,128)(2,1)S(1)} %collective-permute-done.10.refs_2_), channel_id=1, source_target_pairs={{0,1},{1,0},{2,3},{3,2},{4,5},{5,4},{6,7},{7,6},{8,9},{9,8},{10,11... | collective-permute-start | bytes 4644872 | tf_op jit(solution)/shard_map/ppermute | solution.py:401
  320.7 70.7 %copy-start.1 = (bf16[3,112,2304]{2,1,0:T(8,128)(2,1)}, bf16[3,112,2304]{2,1,0:T(8,128)(2,1)S(1)}, u32[]{:S(2)}) copy-start(bf16[3,112,2304]{2,1,0:T(8,128)(2,1)S(1)} %collective-permute-done.1.refs_2_) | copy-start | bytes 4644868
  320.7 29.3 %collective-permute-start.11 = (bf16[3,112,1152]{2,1,0:T(8,128)(2,1)S(1)}, bf16[3,112,1152]{2,1,0:T(8,128)(2,1)S(1)}, u32[]{:S(2)}, u32[]{:S(2)}) collective-permute-start(bf16[3,112,1152]{2,1,0:T(8,128)(2,1)S(1)} %slice.18), channel_id=1, source_target_pairs={{0,2},{1,3},{2,4},{3,5},{4,6},{5,7},{6,0},{7,1},{8,10},{9,11},{10,... | collective-permute-start | bytes 2322440 | tf_op jit(solution)/shard_map/ppermute | solution.py:401
  320.7 37.0 %copy-start.4 = (bf16[3,112,2304]{2,1,0:T(8,128)(2,1)}, bf16[3,112,2304]{2,1,0:T(8,128)(2,1)S(1)}, u32[]{:S(2)}) copy-start(bf16[3,112,2304]{2,1,0:T(8,128)(2,1)S(1)} %collective-permute-done.13.refs_5_) | copy-start | bytes 4644868
  320.7 29.3 %collective-permute-start.12 = (bf16[3,112,1152]{2,1,0:T(8,128)(2,1)S(1)}, bf16[3,112,1152]{2,1,0:T(8,128)(2,1)S(1)}, u32[]{:S(2)}, u32[]{:S(2)}) collective-permute-start(bf16[3,112,1152]{2,1,0:T(8,128)(2,1)S(1)} %slice.19), channel_id=1, source_target_pairs={{0,6},{1,7},{2,0},{3,1},{4,2},{5,3},{6,4},{7,5},{8,14},{9,15},{10,... | collective-permute-start | bytes 2322440 | tf_op jit(solution)/shard_map/ppermute | solution.py:401
  336.5 54.9 %copy-start.7 = (bf16[3,112,1152]{2,1,0:T(8,128)(2,1)}, bf16[3,112,1152]{2,1,0:T(8,128)(2,1)S(1)}, u32[]{:S(2)}) copy-start(bf16[3,112,1152]{2,1,0:T(8,128)(2,1)S(1)} %collective-permute-done.2.refs_3_) | copy-start | bytes 2322436
  336.5 20.6 %collective-permute-start.3 = (bf16[3,112,1152]{2,1,0:T(8,128)(2,1)S(1)}, bf16[3,112,1152]{2,1,0:T(8,128)(2,1)}, u32[]{:S(2)}, u32[]{:S(2)}) collective-permute-start(bf16[3,112,1152]{2,1,0:T(8,128)(2,1)S(1)} %slice.17), channel_id=1, source_target_pairs={{0,6},{1,7},{2,0},{3,1},{4,2},{5,3},{6,4},{7,5},{8,14},{9,15},{10,... | collective-permute-start | bytes 2322440 | tf_op jit(solution)/shard_map/ppermute | solution.py:401
  350.0 8.8 %copy-start.8 = (bf16[3,112,1152]{2,1,0:T(8,128)(2,1)}, bf16[3,112,1152]{2,1,0:T(8,128)(2,1)S(1)}, u32[]{:S(2)}) copy-start(bf16[3,112,1152]{2,1,0:T(8,128)(2,1)S(1)} %collective-permute-done.11.refs_3_) | copy-start | bytes 2322436
  350.0 7.7 %collective-permute-start.16 = (bf16[3,112,1152]{2,1,0:T(8,128)(2,1)S(1)}, bf16[3,112,1152]{2,1,0:T(8,128)(2,1)S(1)}, u32[]{:S(2)}, u32[]{:S(2)}) collective-permute-start(bf16[3,112,1152]{2,1,0:T(8,128)(2,1)S(1)} %collective-permute-done.11.refs_3_), channel_id=1, source_target_pairs={{0,1},{1,0},{2,3},{3,2},{4,5},{5,4},{6,7},{7,6},{8,9},{9,8},{10,11... | collective-permute-start | bytes 2322440 | tf_op jit(solution)/shard_map/ppermute | solution.py:401
  350.0 8.8 %copy-start.9 = (bf16[3,112,1152]{2,1,0:T(8,128)(2,1)}, bf16[3,112,1152]{2,1,0:T(8,128)(2,1)S(1)}, u32[]{:S(2)}) copy-start(bf16[3,112,1152]{2,1,0:T(8,128)(2,1)S(1)} %collective-permute-done.12.refs_4_) | copy-start | bytes 2322436
  350.0 8.7 %collective-permute-start.17 = (bf16[3,112,1152]{2,1,0:T(8,128)(2,1)S(1)}, bf16[3,112,1152]{2,1,0:T(8,128)(2,1)S(1)}, u32[]{:S(2)}, u32[]{:S(2)}) collective-permute-start(bf16[3,112,1152]{2,1,0:T(8,128)(2,1)S(1)} %collective-permute-done.12.refs_4_), channel_id=1, source_target_pairs={{0,1},{1,0},{2,3},{3,2},{4,5},{5,4},{6,7},{7,6},{8,9},{9,8},{10,11... | collective-permute-start | bytes 2322440 | tf_op jit(solution)/shard_map/ppermute | solution.py:401
  357.1 51.6 %collective-permute-start.4 = (bf16[3,112,2304]{2,1,0:T(8,128)(2,1)}, bf16[3,112,2304]{2,1,0:T(8,128)(2,1)}, u32[]{:S(2)}, u32[]{:S(2)}) collective-permute-start(bf16[3,112,2304]{2,1,0:T(8,128)(2,1)} %gradients.3.refs_0_), channel_id=1, source_target_pairs={{0,1},{1,0},{2,3},{3,2},{4,5},{5,4},{6,7},{7,6},{8,9},{9,8},{10,11... | collective-permute-start | bytes 4644872 | tf_op jit(solution)/shard_map/ppermute | solution.py:401
  357.1 1.1 copy-start.5
  357.1 51.6 %collective-permute-start.5 = (bf16[3,112,2304]{2,1,0:T(8,128)(2,1)S(1)}, bf16[3,112,2304]{2,1,0:T(8,128)(2,1)}, u32[]{:S(2)}, u32[]{:S(2)}) collective-permute-start(bf16[3,112,2304]{2,1,0:T(8,128)(2,1)S(1)} %collective-permute-done.refs_1_), channel_id=1, source_target_pairs={{0,1},{1,0},{2,3},{3,2},{4,5},{5,4},{6,7},{7,6},{8,9},{9,8},{10,11... | collective-permute-start | bytes 4644872 | tf_op jit(solution)/shard_map/ppermute | solution.py:401
  357.6 1.2 copy-start.6
  357.6 51.1 %collective-permute-start.6 = (bf16[3,112,2304]{2,1,0:T(8,128)(2,1)S(1)}, bf16[3,112,2304]{2,1,0:T(8,128)(2,1)}, u32[]{:S(2)}, u32[]{:S(2)}) collective-permute-start(bf16[3,112,2304]{2,1,0:T(8,128)(2,1)S(1)} %collective-permute-done.1.refs_2_), channel_id=1, source_target_pairs={{0,1},{1,0},{2,3},{3,2},{4,5},{5,4},{6,7},{7,6},{8,9},{9,8},{10,11... | collective-permute-start | bytes 4644872 | tf_op jit(solution)/shard_map/ppermute | solution.py:401
  358.2 0.9 copy-start.10
  358.2 50.5 %collective-permute-start.7 = (bf16[3,112,1152]{2,1,0:T(8,128)(2,1)S(1)}, bf16[3,112,1152]{2,1,0:T(8,128)(2,1)}, u32[]{:S(2)}, u32[]{:S(2)}) collective-permute-start(bf16[3,112,1152]{2,1,0:T(8,128)(2,1)S(1)} %collective-permute-done.2.refs_3_), channel_id=1, source_target_pairs={{0,1},{1,0},{2,3},{3,2},{4,5},{5,4},{6,7},{7,6},{8,9},{9,8},{10,11... | collective-permute-start | bytes 2322440 | tf_op jit(solution)/shard_map/ppermute | solution.py:401
  359.1 0.9 copy-start.11
  360.0 48.8 %collective-permute-start.8 = (bf16[3,112,1152]{2,1,0:T(8,128)(2,1)}, bf16[3,112,1152]{2,1,0:T(8,128)(2,1)}, u32[]{:S(2)}, u32[]{:S(2)}) collective-permute-start(bf16[3,112,1152]{2,1,0:T(8,128)(2,1)} %collective-permute-done.3.refs_4_), channel_id=1, source_target_pairs={{0,1},{1,0},{2,3},{3,2},{4,5},{5,4},{6,7},{7,6},{8,9},{9,8},{10,11... | collective-permute-start | bytes 2322440 | tf_op jit(solution)/shard_map/ppermute | solution.py:401

commit v2 on v1

--- a/solution.py
+++ b/solution.py
@@ -68,16 +68,14 @@
     )(h, wg, wu, wd)
 
 
-PAIRED, PASSED, ARRIVED = 3, 6, 9
-
-
-def gradients_kernel(size, tile, known, h_ref, dy_ref, gate_ref, up_ref, wd_ref, o_ref, *refs):
-    *kept, x, y, g, pr, p, r1a, r1b, r2a, r2b, send, recv = refs
+PAIRED, PASSED, ARRIVED = 3, 6, 12
+
+
+def gradients_kernel(size, tile, known, h_ref, dy_ref, gate_ref, up_ref, wd_ref, oa_ref, ob_ref, *refs):
+    *kept, a, dy, x, y, g, pr, p, r1a, r1b, r2a, r2b, send, recv, load = refs
     tokens = h_ref.shape[0]
-    if not known:
-        *kept, a = kept
     step = pl.program_id(0)
-    steps = pl.num_programs(0) - ARRIVED // 3
+    steps = pl.num_programs(0) - pl.cdiv(ARRIVED, 3)
     pieces = 3 * steps
     slots = g.shape[0]
     rows = g.shape[1] // size
@@ -89,6 +87,11 @@
     partner = me + 1 - 2 * core
     right, left = lax.rem(me + 2, size), lax.rem(me + size - 2, size)
 
+    def inputs(i):
+        t = pl.ds(i, tile)
+        pairs = enumerate(((h_ref, a), (dy_ref, dy)))
+        return [pltpu.make_async_copy(source.at[t], target.at[t], load.at[which, i // tile]) for which, (source, target) in pairs]
+
     def of_chip(offset):
         return pl.ds(pl.multiple_of(lax.rem(chip + offset, quarters) * rows, 16), rows)
 
@@ -117,15 +120,19 @@
 
     @pl.when(step == 0)
     def _():
+        for i in range(0, tokens, tile):
+            for one in inputs(i):
+                one.start()
         barrier = pltpu.get_barrier_semaphore()
         for device in (partner, left, right):
             pl.semaphore_signal(barrier, inc=1, device_id={"dp": device}, device_id_type=pl.DeviceIdType.MESH)
         pl.semaphore_wait(barrier, 3)
         for i in range(0, tokens, tile):
-            part = normed(h_ref[i : i + tile].astype(F32))
-            if not known:
-                a[i : i + tile] = part
-            x[0, :, i : i + tile] = dy_ref[i : i + tile].T
+            for one in inputs(i):
+                one.wait()
+            part = normed(a[i : i + tile].astype(F32))
+            a[i : i + tile] = part
+            x[0, :, i : i + tile] = dy[i : i + tile].T
             x[1, :, i : i + tile] = part.T
 
     @pl.when(step < steps)
@@ -133,7 +140,7 @@
         for i in range(0, tokens, tile):
             t = slice(i, i + tile)
             gate, up = (gate_ref[t], up_ref[t]) if known else (mm(a[t], gate_ref[...]), mm(a[t], up_ref[...]))
-            by_hid = mm(dy_ref[t], wd_ref[...], 1, 1).astype(BF16).astype(F32)
+            by_hid = mm(dy[t], wd_ref[...], 1, 1).astype(BF16).astype(F32)
             s = sigmoid(gate)
             silu = gate * s
             y[0, t] = (silu * up).astype(BF16)
@@ -144,6 +151,8 @@
             if kept:
                 kept[0][0, t] = dg
                 kept[0][1, t] = du
+        for which in range(3):
+            g[lax.rem(3 * step + which, slots)] = mm(x[min(which, 1)], y[which]).astype(BF16)
 
     @pl.loop(0, 3)
     def _(which):
@@ -151,10 +160,6 @@
 
         def stage(after):
             return pl.when((k >= after) & (k < pieces + after))
-
-        @stage(0)
-        def _():
-            g[lax.rem(k, slots)] = mm(x[jnp.minimum(which, 1)], y[which]).astype(BF16)
 
         @stage(PAIRED)
         def _():
@@ -176,26 +181,32 @@
             for one in second(j):
                 one.wait()
             total = (p[j, of_chip(0)].astype(F32) + r2a[j].astype(F32) + r2b[j].astype(F32)).astype(BF16)
-            o_ref[lax.rem(j + 2, 3), :, pl.ds(pl.multiple_of((j // 3) * width, 128), width)] = total
+            for o_ref, first_step in ((oa_ref, 0), (ob_ref, steps // 2)):
+                here = (j // 3 - first_step) * width
+
+                @pl.when((here >= 0) & (here < o_ref.shape[2]))
+                def _(o_ref=o_ref, here=here):
+                    o_ref[lax.rem(j + 2, 3), :, pl.ds(pl.multiple_of(here, 128), width)] = total
+
+        @stage(0)
+        def _():
+            to_partner(k).start()
+
+        @stage(PAIRED)
+        def _():
+            for one in first(k - PAIRED):
+                one.start()
 
         @stage(PASSED)
         def _():
             for one in second(k - PASSED):
                 one.start()
-
-        @stage(PAIRED)
-        def _():
-            for one in first(k - PAIRED):
-                one.start()
-
-        @stage(0)
-        def _():
-            to_partner(k).start()
 
 
 def gradients(size, number, h, dy, known, wg, wu, wd, keep, width=256, tile=512):
     tokens, d = h.shape
     ff = wg.shape[2]
+    tile = tile // 2 if known else tile
     steps, rows, half = ff // width, d // size, d // 2
     pieces = 3 * steps
 
@@ -206,22 +217,24 @@
         column, pair = pl.BlockSpec((tokens, width), lambda k: (0, now(k))), known
     else:
         column, pair = pl.BlockSpec((None, d, width), lambda k: (number, 0, now(k))), (wg, wu)
-    out_specs, out_shape = [whole((3, rows, ff))], [jax.ShapeDtypeStruct((3, rows, ff), BF16)]
+    parts = [(3, rows, count * width) for count in (steps // 2, steps - steps // 2)]
+    out_specs, out_shape = [whole(one) for one in parts], [jax.ShapeDtypeStruct(one, BF16) for one in parts]
     if keep:
         out_specs += [pl.BlockSpec((2, tokens, width), lambda k: (0, 0, now(k)))]
         out_shape += [jax.ShapeDtypeStruct((2, tokens, ff), BF16)]
     return pl.pallas_call(
         functools.partial(gradients_kernel, size, tile, bool(known)),
         name="gradients",
-        grid=(steps + ARRIVED // 3,),
-        in_specs=[whole((tokens, d))] * 2 + [column, column, pl.BlockSpec((None, width, d), lambda k: (number, now(k), 0))],
+        grid=(steps + pl.cdiv(ARRIVED, 3),),
+        in_specs=[pl.BlockSpec(memory_space=pltpu.HBM)] * 2 + [column, column, pl.BlockSpec((None, width, d), lambda k: (number, now(k), 0))],
         out_specs=out_specs,
         out_shape=out_shape,
         scratch_shapes=[
-            *([] if known else [pltpu.VMEM((tokens, d), BF16)]),
+            pltpu.VMEM((tokens, d), BF16),
+            pltpu.VMEM((tokens, d), BF16),
             pltpu.VMEM((2, d, tokens), BF16),
             pltpu.VMEM((3, tokens, width), BF16),
-            pltpu.VMEM((PAIRED + 1, d, width), BF16),
+            pltpu.VMEM((PAIRED + 3, d, width), BF16),
             pltpu.VMEM((pieces, half, width), BF16),
             pltpu.VMEM((pieces, half, width), BF16),
             pltpu.VMEM((pieces, rows, width // 2), BF16),
@@ -230,6 +243,7 @@
             pltpu.VMEM((pieces, rows, width), BF16),
             pltpu.SemaphoreType.DMA((5, pieces)),
             pltpu.SemaphoreType.DMA((5, pieces)),
+            pltpu.SemaphoreType.DMA((2, tokens // tile)),
         ],
         compiler_params=PARAMS(collective_id=number, has_side_effects=True),
         cost_estimate=cost((8 if known else 12) * tokens * d * ff, 2 * (2 * tokens * d + 2 * tokens * ff + 6 * d * ff)),
@@ -245,7 +259,7 @@
     o_ref[...] = (dy_ref[...].astype(F32) + by_h.astype(BF16).astype(F32)).astype(BF16)
 
 
-def back(number, h, dy, y, wg, wu, tile=512):
+def back(number, h, dy, y, wg, wu, tile=256):
     tokens, d = h.shape
     ff = wg.shape[2]
     row = pl.BlockSpec((tile, d), lambda i: (i, 0))
@@ -262,16 +276,17 @@
     )(h, dy, y, y, wg, wu)
 
 
-FLIGHT = 3
+FLIGHT = 4
 
 
 def adamw_kernel(number, first, count, blocks, size, turned, aliased, *refs):
-    parts, refs = refs[:10], refs[10:]
+    parts, refs = refs[:16], refs[16:]
     sources, refs = refs[: 3 * count], refs[3 * count + aliased :]
     targets, refs = refs[: 3 * count], refs[3 * count :]
     g_buf, wi, mi, vi, wo, mo, vo, g_sem, in_sem, out_sem = refs
     rows, per = wi.shape[1], blocks // count
-    shard, middle = parts[0].shape[1], parts[3].shape[2]
+    shard = parts[0].shape[1]
+    middle, rest = parts[0].shape[2], parts[1].shape[2]
     quarters = size // 2
     me = lax.axis_index("dp")
     core, chip = lax.rem(me, 2), me // 2
@@ -283,13 +298,14 @@
         return side * quarters + lax.rem(chip + offset, quarters)
 
     def of_shard(which, matrix, target, sem):
-        group, at = parts[5 * (which // 4) :], which % 4
-        if at < 3:
-            return [pltpu.make_async_copy(group[at].at[matrix], target, sem)]
+        a, b = parts[2 * which : 2 * which + 2]
         return [
-            pltpu.make_async_copy(group[3].at[matrix], target.at[:, pl.ds(0, middle)], sem),
-            pltpu.make_async_copy(group[4].at[matrix], target.at[:, pl.ds(middle, middle)], sem),
+            pltpu.make_async_copy(a.at[matrix], target.at[:, pl.ds(0, middle)], sem),
+            pltpu.make_async_copy(b.at[matrix], target.at[:, pl.ds(middle, rest)], sem),
         ]
+
+    def arrived(target, sem):
+        pltpu.make_async_copy(target, target, sem).wait()
 
     def move(c, arrays, buffers, sem, into):
         slot, block = lax.rem(c, FLIGHT), lax.rem(c, per)
@@ -317,7 +333,7 @@
             far, near = arrays[kind * count].at[number, pl.ds(0, rows)], buffers[kind].at[slot]
             pltpu.make_async_copy(*((far, near) if into else (near, far)), sem.at[kind, slot]).wait()
         if into and not turned:
-            pltpu.make_async_copy(parts[0].at[first], g_buf.at[slot], g_sem.at[slot]).wait()
+            arrived(g_buf.at[slot], g_sem.at[slot])
 
     def fetch(c):
         move(c, sources, (wi, mi, vi), in_sem, True)
@@ -330,7 +346,7 @@
         fetch(c)
     if turned:
         for which in range(8):
-            pltpu.make_async_copy(parts[0].at[first], g_buf.at[pl.ds(0, shard)], g_sem.at[which]).wait()
+            arrived(g_buf.at[pl.ds(0, shard)], g_sem.at[which])
 
     @pl.loop(0, blocks)
     def _(c):
@@ -361,12 +377,12 @@
 
 def adamw(size, number, first, parts, weights, moments, squares, turned, so_far, width=256):
     count = len(weights)
-    shard, ff = parts[0].shape[1:]
+    shard, ff = parts[0].shape[1], parts[0].shape[2] + parts[1].shape[2]
     d = shard * size
     so_far = so_far or ()
     rows, columns = (width, d) if turned else (shard, ff)
     blocks = count * weights[0].shape[1] // rows
-    hbm = pl.BlockSpec(memory_space=pl.ANY)
+    hbm = pl.BlockSpec(memory_space=pltpu.HBM)
     inputs = (*parts, *weights, *moments, *squares, *so_far)
     return pl.pallas_call(
         functools.partial(adamw_kernel, number, first, count, blocks, size, turned, len(so_far)),
@@ -381,7 +397,7 @@
             pltpu.SemaphoreType.DMA((3, FLIGHT)),
             pltpu.SemaphoreType.DMA((3, FLIGHT)),
         ],
-        input_output_aliases={10 + 3 * count + i: i for i in range(len(so_far))},
+        input_output_aliases={16 + 3 * count + i: i for i in range(len(so_far))},
         compiler_params=PARAMS(),
         cost_estimate=cost(count * 5 * 2048 * d * ff // 2, count * 22 * d * ff),
     )(*inputs)
@@ -400,14 +416,12 @@
         def hop(one, to):
             return lax.ppermute(one, "dp", to)
 
-        def gathered(own):
-            middle = own.shape[2] // 2
-            left, right = hop(own, to_right), hop(own, to_left)
-            first = hop(left[:, :, :middle], to_right)
-            second = hop(right[:, :, middle:], to_left)
-            pairs = [hop(own, swap), hop(left, swap), hop(right, swap)]
-            pairs += [hop(first, swap), hop(second, swap)]
-            return (own, left, right, first, second, *pairs)
+        def gathered(a, b):
+            near, far, last = (hop for _ in range(3))
+            mine = [a, b, near(a, to_right), near(b, to_right), near(a, to_left), near(b, to_left)]
+            mine += [far(mine[2], to_right), far(mine[5], to_left)]
+            hops = (near, near, far, far, far, far, last, last)
+            return (*mine, *(by(one, swap) for by, one in zip(hops, mine, strict=True)))
 
         h, kept, known = x[0], [], []
         for number in range(layers):
@@ -418,8 +432,8 @@
             known.append(both)
         by_h, every = dy[0], []
         for number in reversed(range(layers)):
-            own, *by_both = gradients(size, number, kept[number], by_h, known[number], *weights, number > 0)
-            every.append((number, gathered(own)))
+            a, b, *by_both = gradients(size, number, kept[number], by_h, known[number], *weights, number > 0)
+            every.append((number, gathered(a, b)))
             if number:
                 by_h = back(number, kept[number], by_h, by_both[0], *weights[:2])
         side, down = None, None

time: 457 us -> 431 us (0.943)
  waiting for transfers between devices: 97.8 us -> 74.6 us
  Pallas kernels: 344 us -> 332 us
  starting transfers between devices: 12.2 us -> 19.4 us
    ppermute x18 -> x28, waiting for transfers between devices: 97.8 us -> 74.6 us  [hop(): return lax.ppermute(one, 'dp', to)]
    pallas_call x2, Pallas kernels: 181 us -> 171 us  [gradients(): pl.pallas_call(functools.partial(gradients_kernel, size, tile, bool(known...]
    ppermute x18 -> x28, starting transfers between devices: 12.2 us -> 19.4 us  [hop(): return lax.ppermute(one, 'dp', to)]
  transfers between devices with their start and end apart: 18 -> 28, of which waited for: 5 -> 7; matrix products, arithmetic and copies ran while one was open for 0% -> 0% of each run, Pallas kernels for 11% -> 11%
where the time goes in v2:
time: 431 us
  Pallas kernels  332 us (77%)
  waiting for transfers between devices  74.6 us (17%)
  starting transfers between devices  19.4 us (5%)
    pallas_call x2, Pallas kernels, gradients(): pl.pallas_call(functools.partial(gradients_kernel, size, tile, bool(known...  171 us
    pallas_call x4, Pallas kernels, adamw(): pl.pallas_call(functools.partial(adamw_kernel, number, first, count, bloc...  95.5 us
    ppermute x28, waiting for transfers between devices, hop(): return lax.ppermute(one, 'dp', to)  74.6 us
    pallas_call x1, Pallas kernels, forward(): pl.pallas_call(functools.partial(forward_kernel, width), name='forward',...  37.4 us
    pallas_call x1, Pallas kernels, back(): pl.pallas_call(back_kernel, name='back', grid=(tokens // tile,), in_specs...  28.9 us
    ppermute x28, starting transfers between devices, hop(): return lax.ppermute(one, 'dp', to)  19.4 us
  transfers between devices with their start and end apart: 28, of which 7 were waited for; matrix products, arithmetic and copies ran while one was open for 0% of the time, Pallas kernels for 11%

profile of v2, /device:TPU:112, one launch (start us, length us, event | category | flops | bytes accessed | tf_op | source)
XLA Modules:
  0.0 430.8 jit_solution(14461234502871757179)
XLA Ops:
  0.6 37.4 %forward.1 = (bf16[2048,896]{1,0:T(8,128)(2,1)}, f32[2048,2304]{1,0:T(8,128)}, f32[2048,2304]{1,0:T(8,128)}) custom-call(bf16[2048,896]{1,0:T(8,128)(2,1)} %bitcast.4, bf16[2,896,2304]{2,1,0:T(8,128)(2,1)} %refs_16_.5, bf16[2,896,2304]{2,1,0:T(8,128)(2,1)} %refs_17_.5, bf16[2,2304,896]{2,1,0:T(8,128)(2,1)} %refs_16_.7), custom_call_target="tpu_custom_call" | custom-call | flops 25367150592 | bytes 57475072 | tf_op jit(solution)/shard_map/forward/pallas_call | solution.py:58
  38.0 94.8 %gradients.2 = (bf16[3,112,1024]{2,1,0:T(8,128)(2,1)}, bf16[3,112,1280]{2,1,0:T(8,128)(2,1)}, bf16[2,2048,2304]{2,1,0:T(8,128)(2,1)}) custom-call(bf16[2048,896]{1,0:T(8,128)(2,1)} %get-tuple-element.35.h_ref, bf16[2048,896]{1,0:T(8,128)(2,1)} %bitcast.2, bf16[2,896,2304]{2,1,0:T(8,128)(2,1)} %refs_16_.5, bf16[2,896,2304]{2,1,0:T(8,128)(2,1)} %refs_17_.5, ...), custom_call_target="tpu_custom_call" | custom-call | flops 50734301184 | bytes 50987008 | tf_op jit(solution)/shard_map/gradients/pallas_call | solution.py:225
  132.8 28.9 %back.1.dy_ref = bf16[2048,896]{1,0:T(8,128)(2,1)} custom-call(bf16[2048,896]{1,0:T(8,128)(2,1)} %get-tuple-element.35.h_ref, bf16[2048,896]{1,0:T(8,128)(2,1)} %bitcast.3, bf16[2,2048,2304]{2,1,0:T(8,128)(2,1)} %get-tuple-element.36.dg_ref.du_ref, bf16[2,2048,2304]{2,1,0:T(8,128)(2,1)} %get-tuple-element.36.dg_ref.du_ref, bf16[2,896,2304]{2,1,0:T(8,128)(2,1)} %refs_16_.5, ...), custom_call_target="tpu_custom_call" | custom-call | flops 16911433728 | bytes 38141952 | tf_op jit(solution)/shard_map/back/pallas_call | solution.py:267
  161.7 75.8 %gradients.3 = (bf16[3,112,1024]{2,1,0:T(8,128)(2,1)}, bf16[3,112,1280]{2,1,0:T(8,128)(2,1)}) custom-call(bf16[2048,896]{1,0:T(8,128)(2,1)} %bitcast.5, bf16[2048,896]{1,0:T(8,128)(2,1)} %back.1.dy_ref, f32[2048,2304]{1,0:T(8,128)} %get-tuple-element.37.gate_ref, f32[2048,2304]{1,0:T(8,128)} %get-tuple-element.38.up_ref, bf16[2,2304,896]{2,1,0:T(8,128)(2,1)} %refs_16_.7), custom_call_target="tpu_custom_call" | custom-call | flops 33822867456 | bytes 50987008 | tf_op jit(solution)/shard_map/gradients/pallas_call | solution.py:225
  237.5 0.6 collective-permute-start
  238.2 2.7 collective-permute-start.2
  240.9 0.6 collective-permute-start.17
  241.4 1.5 collective-permute-start.14
  242.9 14.5 %collective-permute-done.refs_2_ = bf16[3,112,1024]{2,1,0:T(8,128)(2,1)S(1)} collective-permute-done((bf16[3,112,1024]{2,1,0:T(8,128)(2,1)}, bf16[3,112,1024]{2,1,0:T(8,128)(2,1)S(1)}, u32[]{:S(2)}, u32[]{:S(2)}) %collective-permute-start) | collective-permute-done | bytes 688160 | tf_op jit(solution)/shard_map/ppermute | solution.py:417
  257.4 0.6 collective-permute-start.16
  257.9 0.9 copy-done.13
  258.8 2.7 collective-permute-start.3
  261.5 0.8 copy-done.14
  262.3 6.5 %collective-permute-done.14.refs_2_ = bf16[3,112,1024]{2,1,0:T(8,128)(2,1)S(1)} collective-permute-done((bf16[3,112,1024]{2,1,0:T(8,128)(2,1)S(1)}, bf16[3,112,1024]{2,1,0:T(8,128)(2,1)S(1)}, u32[]{:S(2)}, u32[]{:S(2)}) %collective-permute-start.14) | collective-permute-done | bytes 688160 | tf_op jit(solution)/shard_map/ppermute | solution.py:417
  268.8 21.3 %collective-permute-done.16.refs_4_ = bf16[3,112,1024]{2,1,0:T(8,128)(2,1)S(1)} collective-permute-done((bf16[3,112,1024]{2,1,0:T(8,128)(2,1)S(1)}, bf16[3,112,1024]{2,1,0:T(8,128)(2,1)S(1)}, u32[]{:S(2)}, u32[]{:S(2)}) %collective-permute-start.16) | collective-permute-done | bytes 688160 | tf_op jit(solution)/shard_map/ppermute | solution.py:417
  290.1 3.8 collective-permute-start.19
  293.9 14.7 %collective-permute-done.3.refs_5_ = bf16[3,112,1280]{2,1,0:T(8,128)(2,1)S(1)} collective-permute-done((bf16[3,112,1280]{2,1,0:T(8,128)(2,1)}, bf16[3,112,1280]{2,1,0:T(8,128)(2,1)S(1)}, u32[]{:S(2)}, u32[]{:S(2)}) %collective-permute-start.3) | collective-permute-done | bytes 860192 | tf_op jit(solution)/shard_map/ppermute | solution.py:417
  308.6 0.6 collective-permute-start.23
  309.3 14.3 %collective-permute-done.19.refs_7_ = bf16[3,112,1280]{2,1,0:T(8,128)(2,1)S(1)} collective-permute-done((bf16[3,112,1280]{2,1,0:T(8,128)(2,1)S(1)}, bf16[3,112,1280]{2,1,0:T(8,128)(2,1)S(1)}, u32[]{:S(2)}, u32[]{:S(2)}) %collective-permute-start.19) | collective-permute-done | bytes 860192 | tf_op jit(solution)/shard_map/ppermute | solution.py:417
  324.2 2.8 collective-permute-done.24.refs_12_
  327.0 0.9 collective-permute-start.1
  327.9 1.8 collective-permute-start.4
  330.0 0.6 copy-done.22
  330.6 0.9 copy-done.11
  331.5 1.7 collective-permute-start.5
  333.2 30.5 %adamw.4 = (bf16[2,896,2304]{2,1,0:T(8,128)(2,1)}, bf16[2,896,2304]{2,1,0:T(8,128)(2,1)}, f32[2,896,2304]{2,1,0:T(8,128)}, f32[2,896,2304]{2,1,0:T(8,128)}, f32[...) custom-call(bf16[3,112,1024]{2,1,0:T(8,128)(2,1)} %get-tuple-element.41.refs_0_, ...), custom_call_target="tpu_custom_call" | custom-call | flops 21139292160 | bytes 90832896 | tf_op jit(solution)/shard_map/adamw/pallas_call | solution.py:387
  363.8 0.5 collective-permute-start.11
  364.3 0.6 collective-permute-done.4.refs_6_
  364.9 0.5 collective-permute-start.12
  365.5 17.4 %adamw.6 = (bf16[2,2304,896]{2,1,0:T(8,128)(2,1)}, f32[2,2304,896]{2,1,0:T(8,128)}, f32[2,2304,896]{2,1,0:T(8,128)}) custom-call(bf16[3,112,1024]{2,1,0:T(8,128)(2,1)} %get-tuple-element.41.refs_0_, bf16[3,112,1280]{2,1,0:T(8,128)(2,1)} %get-tuple-element.42.refs_1_, bf16[3,112,1024]{2,1,0:T(8,128)(2,1)} %copy-done.16, bf16[3,112,1280]{2,1,0:T(8,128)(2,1)} %copy-done.6, ...), custom_call_target="tpu_custom_call" | custom-call | flops 10569646080 | bytes 45416448 | tf_op jit(solution)/shard_map/adamw/pallas_call | solution.py:387
  383.0 17.2 %adamw.7 = (bf16[2,2304,896]{2,1,0:T(8,128)(2,1)}, f32[2,2304,896]{2,1,0:T(8,128)}, f32[2,2304,896]{2,1,0:T(8,128)}) custom-call(bf16[3,112,1024]{2,1,0:T(8,128)(2,1)} %get-tuple-element.39.refs_0_, bf16[3,112,1280]{2,1,0:T(8,128)(2,1)} %get-tuple-element.40.refs_1_, ...), custom_call_target="tpu_custom_call", output_to_operand_aliasing={{0}: (19, {}), {1}: (20, {}), {2}: (21, {})} | custom-call | flops 10569646080 | bytes 45416448 | tf_op jit(solution)/shard_map/adamw/pallas_call | solution.py:387
  400.2 30.5 %adamw.5 = (bf16[2,896,2304]{2,1,0:T(8,128)(2,1)}, bf16[2,896,2304]{2,1,0:T(8,128)(2,1)}, f32[2,896,2304]{2,1,0:T(8,128)}, f32[2,896,2304]{2,1,0:T(8,128)}, f32[...) custom-call(bf16[3,112,1024]{2,1,0:T(8,128)(2,1)} %get-tuple-element, ...), custom_call_target="tpu_custom_call", output_to_operand_aliasing={{0}: (22, {}), {1}: (23, {}), {2}: (24, {}), {3}: (25, {}),... | custom-call | flops 21139292160 | bytes 90832896 | tf_op jit(solution)/shard_map/adamw/pallas_call | solution.py:387
  (78 shorter events, 1.2 us)
Async XLA Ops:
  161.7 79.2 %copy-start.4 = (bf16[3,112,1280]{2,1,0:T(8,128)(2,1)S(1)}, bf16[3,112,1280]{2,1,0:T(8,128)(2,1)}, u32[]{:S(2)}) copy-start(bf16[3,112,1280]{2,1,0:T(8,128)(2,1)} %get-tuple-element.42.refs_1_) | copy-start | bytes 2580484
  161.7 79.7 %copy-start.15 = (bf16[3,112,1024]{2,1,0:T(8,128)(2,1)S(1)}, bf16[3,112,1024]{2,1,0:T(8,128)(2,1)}, u32[]{:S(2)}) copy-start(bf16[3,112,1024]{2,1,0:T(8,128)(2,1)} %get-tuple-element.41.refs_0_) | copy-start | bytes 2064388
  237.5 19.8 %collective-permute-start = (bf16[3,112,1024]{2,1,0:T(8,128)(2,1)}, bf16[3,112,1024]{2,1,0:T(8,128)(2,1)S(1)}, u32[]{:S(2)}, u32[]{:S(2)}) collective-permute-start(bf16[3,112,1024]{2,1,0:T(8,128)(2,1)} %get-tuple-element.39.refs_0_), channel_id=1, source_target_pairs={{0,2},{1,3},{2,4},{3,5},{4,6},{5,7},{6,0},{7,1},{8,10},{9,11},{10,... | collective-permute-start | bytes 2064392 | tf_op jit(solution)/shard_map/ppermute | solution.py:417
  238.2 19.8 %collective-permute-start.2 = (bf16[3,112,1024]{2,1,0:T(8,128)(2,1)}, bf16[3,112,1024]{2,1,0:T(8,128)(2,1)S(1)}, u32[]{:S(2)}, u32[]{:S(2)}) collective-permute-start(bf16[3,112,1024]{2,1,0:T(8,128)(2,1)} %get-tuple-element.39.refs_0_), channel_id=1, source_target_pairs={{0,6},{1,7},{2,0},{3,1},{4,2},{5,3},{6,4},{7,5},{8,14},{9,15},{10,... | collective-permute-start | bytes 2064392 | tf_op jit(solution)/shard_map/ppermute | solution.py:417
  240.9 20.6 %collective-permute-start.6 = (bf16[3,112,1024]{2,1,0:T(8,128)(2,1)}, bf16[3,112,1024]{2,1,0:T(8,128)(2,1)S(1)}, u32[]{:S(2)}, u32[]{:S(2)}) collective-permute-start(bf16[3,112,1024]{2,1,0:T(8,128)(2,1)} %get-tuple-element.39.refs_0_), channel_id=1, source_target_pairs={{0,1},{1,0},{2,3},{3,2},{4,5},{5,4},{6,7},{7,6},{8,9},{9,8},{10,11... | collective-permute-start | bytes 2064392 | tf_op jit(solution)/shard_map/ppermute | solution.py:417
  240.9 49.2 %collective-permute-start.17 = (bf16[3,112,1280]{2,1,0:T(8,128)(2,1)S(1)}, bf16[3,112,1280]{2,1,0:T(8,128)(2,1)S(1)}, u32[]{:S(2)}, u32[]{:S(2)}) collective-permute-start(bf16[3,112,1280]{2,1,0:T(8,128)(2,1)S(1)} %copy-done.4), channel_id=1, source_target_pairs={{0,6},{1,7},{2,0},{3,1},{4,2},{5,3},{6,4},{7,5},{8,14},{9,15},{10,... | collective-permute-start | bytes 2580488 | tf_op jit(solution)/shard_map/ppermute | solution.py:417
  241.4 27.3 %collective-permute-start.14 = (bf16[3,112,1024]{2,1,0:T(8,128)(2,1)S(1)}, bf16[3,112,1024]{2,1,0:T(8,128)(2,1)S(1)}, u32[]{:S(2)}, u32[]{:S(2)}) collective-permute-start(bf16[3,112,1024]{2,1,0:T(8,128)(2,1)S(1)} %copy-done.15), channel_id=1, source_target_pairs={{0,2},{1,3},{2,4},{3,5},{4,6},{5,7},{6,0},{7,1},{8,10},{9,11},{10,... | collective-permute-start | bytes 2064392 | tf_op jit(solution)/shard_map/ppermute | solution.py:417
  257.4 125.5 %copy-start.12 = (bf16[3,112,1024]{2,1,0:T(8,128)(2,1)}, bf16[3,112,1024]{2,1,0:T(8,128)(2,1)S(1)}, u32[]{:S(2)}) copy-start(bf16[3,112,1024]{2,1,0:T(8,128)(2,1)S(1)} %collective-permute-done.refs_2_) | copy-start | bytes 2064388
  257.4 32.7 %collective-permute-start.16 = (bf16[3,112,1024]{2,1,0:T(8,128)(2,1)S(1)}, bf16[3,112,1024]{2,1,0:T(8,128)(2,1)S(1)}, u32[]{:S(2)}, u32[]{:S(2)}) collective-permute-start(bf16[3,112,1024]{2,1,0:T(8,128)(2,1)S(1)} %copy-done.15), channel_id=1, source_target_pairs={{0,6},{1,7},{2,0},{3,1},{4,2},{5,3},{6,4},{7,5},{8,14},{9,15},{10,... | collective-permute-start | bytes 2064392 | tf_op jit(solution)/shard_map/ppermute | solution.py:417
  258.8 49.8 %collective-permute-start.3 = (bf16[3,112,1280]{2,1,0:T(8,128)(2,1)}, bf16[3,112,1280]{2,1,0:T(8,128)(2,1)S(1)}, u32[]{:S(2)}, u32[]{:S(2)}) collective-permute-start(bf16[3,112,1280]{2,1,0:T(8,128)(2,1)} %get-tuple-element.40.refs_1_), channel_id=1, source_target_pairs={{0,6},{1,7},{2,0},{3,1},{4,2},{5,3},{6,4},{7,5},{8,14},{9,15},{10,... | collective-permute-start | bytes 2580488 | tf_op jit(solution)/shard_map/ppermute | solution.py:417
  261.5 32.4 %collective-permute-start.20 = (bf16[3,112,1024]{2,1,0:T(8,128)(2,1)S(1)}, bf16[3,112,1024]{2,1,0:T(8,128)(2,1)S(1)}, u32[]{:S(2)}, u32[]{:S(2)}) collective-permute-start(bf16[3,112,1024]{2,1,0:T(8,128)(2,1)S(1)} %copy-done.15), channel_id=1, source_target_pairs={{0,1},{1,0},{2,3},{3,2},{4,5},{5,4},{6,7},{7,6},{8,9},{9,8},{10,11... | collective-permute-start | bytes 2064392 | tf_op jit(solution)/shard_map/ppermute | solution.py:417
  268.8 61.1 %copy-start.16 = (bf16[3,112,1024]{2,1,0:T(8,128)(2,1)}, bf16[3,112,1024]{2,1,0:T(8,128)(2,1)S(1)}, u32[]{:S(2)}) copy-start(bf16[3,112,1024]{2,1,0:T(8,128)(2,1)S(1)} %collective-permute-done.14.refs_2_) | copy-start | bytes 2064388
  268.8 39.8 %collective-permute-start.15 = (bf16[3,112,1280]{2,1,0:T(8,128)(2,1)S(1)}, bf16[3,112,1280]{2,1,0:T(8,128)(2,1)S(1)}, u32[]{:S(2)}, u32[]{:S(2)}) collective-permute-start(bf16[3,112,1280]{2,1,0:T(8,128)(2,1)S(1)} %copy-done.4), channel_id=1, source_target_pairs={{0,2},{1,3},{2,4},{3,5},{4,6},{5,7},{6,0},{7,1},{8,10},{9,11},{10,... | collective-permute-start | bytes 2580488 | tf_op jit(solution)/shard_map/ppermute | solution.py:417
  290.1 19.1 %collective-permute-start.21 = (bf16[3,112,1280]{2,1,0:T(8,128)(2,1)S(1)}, bf16[3,112,1280]{2,1,0:T(8,128)(2,1)S(1)}, u32[]{:S(2)}, u32[]{:S(2)}) collective-permute-start(bf16[3,112,1280]{2,1,0:T(8,128)(2,1)S(1)} %copy-done.4), channel_id=1, source_target_pairs={{0,1},{1,0},{2,3},{3,2},{4,5},{5,4},{6,7},{7,6},{8,9},{9,8},{10,11... | collective-permute-start | bytes 2580488 | tf_op jit(solution)/shard_map/ppermute | solution.py:417
  290.1 33.5 %collective-permute-start.19 = (bf16[3,112,1280]{2,1,0:T(8,128)(2,1)S(1)}, bf16[3,112,1280]{2,1,0:T(8,128)(2,1)S(1)}, u32[]{:S(2)}, u32[]{:S(2)}) collective-permute-start(bf16[3,112,1280]{2,1,0:T(8,128)(2,1)S(1)} %collective-permute-done.17.refs_5_), channel_id=1, source_target_pairs={{0,6},{1,7},{2,0},{3,1},{4,2},{5,3},{6,4},{7,5},{8,14},{9,15},{10,... | collective-permute-start | bytes 2580488 | tf_op jit(solution)/shard_map/ppermute | solution.py:417
  293.9 29.7 %collective-permute-start.18 = (bf16[3,112,1024]{2,1,0:T(8,128)(2,1)S(1)}, bf16[3,112,1024]{2,1,0:T(8,128)(2,1)S(1)}, u32[]{:S(2)}, u32[]{:S(2)}) collective-permute-start(bf16[3,112,1024]{2,1,0:T(8,128)(2,1)S(1)} %collective-permute-done.14.refs_2_), channel_id=1, source_target_pairs={{0,2},{1,3},{2,4},{3,5},{4,6},{5,7},{6,0},{7,1},{8,10},{9,11},{10,... | collective-permute-start | bytes 2064392 | tf_op jit(solution)/shard_map/ppermute | solution.py:417
  308.6 15.5 %collective-permute-start.22 = (bf16[3,112,1024]{2,1,0:T(8,128)(2,1)S(1)}, bf16[3,112,1024]{2,1,0:T(8,128)(2,1)S(1)}, u32[]{:S(2)}, u32[]{:S(2)}) collective-permute-start(bf16[3,112,1024]{2,1,0:T(8,128)(2,1)S(1)} %collective-permute-done.14.refs_2_), channel_id=1, source_target_pairs={{0,1},{1,0},{2,3},{3,2},{4,5},{5,4},{6,7},{7,6},{8,9},{9,8},{10,11... | collective-permute-start | bytes 2064392 | tf_op jit(solution)/shard_map/ppermute | solution.py:417
  308.6 19.3 %collective-permute-start.23 = (bf16[3,112,1280]{2,1,0:T(8,128)(2,1)S(1)}, bf16[3,112,1280]{2,1,0:T(8,128)(2,1)S(1)}, u32[]{:S(2)}, u32[]{:S(2)}) collective-permute-start(bf16[3,112,1280]{2,1,0:T(8,128)(2,1)S(1)} %collective-permute-done.15.refs_3_), channel_id=1, source_target_pairs={{0,1},{1,0},{2,3},{3,2},{4,5},{5,4},{6,7},{7,6},{8,9},{9,8},{10,11... | collective-permute-start | bytes 2580488 | tf_op jit(solution)/shard_map/ppermute | solution.py:417
  309.2 18.7 %collective-permute-start.25 = (bf16[3,112,1280]{2,1,0:T(8,128)(2,1)S(1)}, bf16[3,112,1280]{2,1,0:T(8,128)(2,1)S(1)}, u32[]{:S(2)}, u32[]{:S(2)}) collective-permute-start(bf16[3,112,1280]{2,1,0:T(8,128)(2,1)S(1)} %collective-permute-done.17.refs_5_), channel_id=1, source_target_pairs={{0,1},{1,0},{2,3},{3,2},{4,5},{5,4},{6,7},{7,6},{8,9},{9,8},{10,11... | collective-permute-start | bytes 2580488 | tf_op jit(solution)/shard_map/ppermute | solution.py:417
  323.6 6.3 %collective-permute-start.27 = (bf16[3,112,1280]{2,1,0:T(8,128)(2,1)S(1)}, bf16[3,112,1280]{2,1,0:T(8,128)(2,1)S(1)}, u32[]{:S(2)}, u32[]{:S(2)}) collective-permute-start(bf16[3,112,1280]{2,1,0:T(8,128)(2,1)S(1)} %collective-permute-done.19.refs_7_), channel_id=1, source_target_pairs={{0,1},{1,0},{2,3},{3,2},{4,5},{5,4},{6,7},{7,6},{8,9},{9,8},{10,11... | collective-permute-start | bytes 2580488 | tf_op jit(solution)/shard_map/ppermute | solution.py:417
  323.6 3.4 collective-permute-start.24
  324.1 5.6 %collective-permute-start.26 = (bf16[3,112,1024]{2,1,0:T(8,128)(2,1)S(1)}, bf16[3,112,1024]{2,1,0:T(8,128)(2,1)S(1)}, u32[]{:S(2)}, u32[]{:S(2)}) collective-permute-start(bf16[3,112,1024]{2,1,0:T(8,128)(2,1)S(1)} %collective-permute-done.18.refs_6_), channel_id=1, source_target_pairs={{0,1},{1,0},{2,3},{3,2},{4,5},{5,4},{6,7},{7,6},{8,9},{9,8},{10,11... | collective-permute-start | bytes 2064392 | tf_op jit(solution)/shard_map/ppermute | solution.py:417
  327.0 36.7 %collective-permute-start.1 = (bf16[3,112,1280]{2,1,0:T(8,128)(2,1)}, bf16[3,112,1280]{2,1,0:T(8,128)(2,1)S(1)}, u32[]{:S(2)}, u32[]{:S(2)}) collective-permute-start(bf16[3,112,1280]{2,1,0:T(8,128)(2,1)} %get-tuple-element.40.refs_1_), channel_id=1, source_target_pairs={{0,2},{1,3},{2,4},{3,5},{4,6},{5,7},{6,0},{7,1},{8,10},{9,11},{10,... | collective-permute-start | bytes 2580488 | tf_op jit(solution)/shard_map/ppermute | solution.py:417
  327.9 35.9 %collective-permute-start.7 = (bf16[3,112,1280]{2,1,0:T(8,128)(2,1)}, bf16[3,112,1280]{2,1,0:T(8,128)(2,1)S(1)}, u32[]{:S(2)}, u32[]{:S(2)}) collective-permute-start(bf16[3,112,1280]{2,1,0:T(8,128)(2,1)} %get-tuple-element.40.refs_1_), channel_id=1, source_target_pairs={{0,1},{1,0},{2,3},{3,2},{4,5},{5,4},{6,7},{7,6},{8,9},{9,8},{10,11... | collective-permute-start | bytes 2580488 | tf_op jit(solution)/shard_map/ppermute | solution.py:417
  327.9 37.0 %collective-permute-start.4 = (bf16[3,112,1024]{2,1,0:T(8,128)(2,1)S(1)}, bf16[3,112,1024]{2,1,0:T(8,128)(2,1)}, u32[]{:S(2)}, u32[]{:S(2)}) collective-permute-start(bf16[3,112,1024]{2,1,0:T(8,128)(2,1)S(1)} %collective-permute-done.refs_2_), channel_id=1, source_target_pairs={{0,2},{1,3},{2,4},{3,5},{4,6},{5,7},{6,0},{7,1},{8,10},{9,11},{10,... | collective-permute-start | bytes 2064392 | tf_op jit(solution)/shard_map/ppermute | solution.py:417
  329.7 35.2 %collective-permute-start.8 = (bf16[3,112,1024]{2,1,0:T(8,128)(2,1)S(1)}, bf16[3,112,1024]{2,1,0:T(8,128)(2,1)}, u32[]{:S(2)}, u32[]{:S(2)}) collective-permute-start(bf16[3,112,1024]{2,1,0:T(8,128)(2,1)S(1)} %collective-permute-done.refs_2_), channel_id=1, source_target_pairs={{0,1},{1,0},{2,3},{3,2},{4,5},{5,4},{6,7},{7,6},{8,9},{9,8},{10,11... | collective-permute-start | bytes 2064392 | tf_op jit(solution)/shard_map/ppermute | solution.py:417
  331.5 33.9 %collective-permute-start.5 = (bf16[3,112,1280]{2,1,0:T(8,128)(2,1)S(1)}, bf16[3,112,1280]{2,1,0:T(8,128)(2,1)S(1)}, u32[]{:S(2)}, u32[]{:S(2)}) collective-permute-start(bf16[3,112,1280]{2,1,0:T(8,128)(2,1)S(1)} %collective-permute-done.3.refs_5_), channel_id=1, source_target_pairs={{0,6},{1,7},{2,0},{3,1},{4,2},{5,3},{6,4},{7,5},{8,14},{9,15},{10,... | collective-permute-start | bytes 2580488 | tf_op jit(solution)/shard_map/ppermute | solution.py:417
  363.7 19.2 %collective-permute-start.10 = (bf16[3,112,1024]{2,1,0:T(8,128)(2,1)}, bf16[3,112,1024]{2,1,0:T(8,128)(2,1)}, u32[]{:S(2)}, u32[]{:S(2)}) collective-permute-start(bf16[3,112,1024]{2,1,0:T(8,128)(2,1)} %copy-done.13), channel_id=1, source_target_pairs={{0,1},{1,0},{2,3},{3,2},{4,5},{5,4},{6,7},{7,6},{8,9},{9,8},{10,11... | collective-permute-start | bytes 2064392 | tf_op jit(solution)/shard_map/ppermute | solution.py:417
  363.8 19.1 %collective-permute-start.11 = (bf16[3,112,1280]{2,1,0:T(8,128)(2,1)S(1)}, bf16[3,112,1280]{2,1,0:T(8,128)(2,1)}, u32[]{:S(2)}, u32[]{:S(2)}) collective-permute-start(bf16[3,112,1280]{2,1,0:T(8,128)(2,1)S(1)} %collective-permute-done.3.refs_5_), channel_id=1, source_target_pairs={{0,1},{1,0},{2,3},{3,2},{4,5},{5,4},{6,7},{7,6},{8,9},{9,8},{10,11... | collective-permute-start | bytes 2580488 | tf_op jit(solution)/shard_map/ppermute | solution.py:417
  364.9 18.0 %collective-permute-start.9 = (bf16[3,112,1280]{2,1,0:T(8,128)(2,1)S(1)}, bf16[3,112,1280]{2,1,0:T(8,128)(2,1)}, u32[]{:S(2)}, u32[]{:S(2)}) collective-permute-start(bf16[3,112,1280]{2,1,0:T(8,128)(2,1)S(1)} %collective-permute-done.1.refs_3_), channel_id=1, source_target_pairs={{0,1},{1,0},{2,3},{3,2},{4,5},{5,4},{6,7},{7,6},{8,9},{9,8},{10,11... | collective-permute-start | bytes 2580488 | tf_op jit(solution)/shard_map/ppermute | solution.py:417
  364.9 18.1 %collective-permute-start.12 = (bf16[3,112,1024]{2,1,0:T(8,128)(2,1)}, bf16[3,112,1024]{2,1,0:T(8,128)(2,1)}, u32[]{:S(2)}, u32[]{:S(2)}) collective-permute-start(bf16[3,112,1024]{2,1,0:T(8,128)(2,1)} %collective-permute-done.4.refs_6_), channel_id=1, source_target_pairs={{0,1},{1,0},{2,3},{3,2},{4,5},{5,4},{6,7},{7,6},{8,9},{9,8},{10,11... | collective-permute-start | bytes 2064392 | tf_op jit(solution)/shard_map/ppermute | solution.py:417
  365.4 17.6 %collective-permute-start.13 = (bf16[3,112,1280]{2,1,0:T(8,128)(2,1)S(1)}, bf16[3,112,1280]{2,1,0:T(8,128)(2,1)}, u32[]{:S(2)}, u32[]{:S(2)}) collective-permute-start(bf16[3,112,1280]{2,1,0:T(8,128)(2,1)S(1)} %collective-permute-done.5.refs_7_), channel_id=1, source_target_pairs={{0,1},{1,0},{2,3},{3,2},{4,5},{5,4},{6,7},{7,6},{8,9},{9,8},{10,11... | collective-permute-start | bytes 2580488 | tf_op jit(solution)/shard_map/ppermute | solution.py:417
  (19 other events, 276.4 us)
